TPU v7x, 768 devices: a whole 4x8x12 slice. The times are simulated.
768 devices in a mesh: dp: 96 (over z, y), mp: 8 (over x, core).
Axes of the slice: x: 4, y: 8, z: 12, core: 2. Of those that a mesh axis runs over, the one named last changes fastest.
Arguments:
- clean: bfloat16 [192, 128, 2432], P('dp'), may hold values from -6 to 6
- noise: bfloat16 [192, 128, 2432], P('dp'), may hold values from -6 to 6
- modulation: float32 [192, 7296], P('dp'), may hold values from -3 to 3
- strata: int32 [192], P('dp'), may hold values from 0 to 63
- up_weight: bfloat16 [2432, 5376], P(None, 'mp'), may hold values from -0.125 to 0.125
- down_weight: bfloat16 [5376, 2432], P('mp'), may hold values from -0.078125 to 0.078125
Outputs:
- up_gradient: float32 [5376, 2432], P(('mp', 'dp'))
- loss_value: float32 [], replicated
All inputs are finite; a program needn't handle non-finite values.
Results may differ from a plain program's by a relative error of at most 0.008.
Values may be sent and summed in bfloat16 or wider, within the bound.
No kernel may reach another device: no remote copies, remote signals or barrier semaphores. Data moves between devices by JAX's collectives and lax.ppermute only.
A program may use at most 128 MiB of HBM per device.

v0:
```python
import math

import jax
import jax.numpy as jnp
from jax import lax
from jax.sharding import Mesh
from jax.sharding import PartitionSpec as P

STRATA = 64
MP = ("mp_0", "mp_1")
DP_MP = ("dp_0", "dp_1", "mp_0", "mp_1")
DP = ("dp_0", "dp_1")
MP_DP = ("mp_0", "mp_1", "dp_0", "dp_1")


loss_scale = 1048576.0


def cut_along(array, dim, size):
    before, after = (array.shape[:dim], array.shape[dim + 1 :])
    return jnp.moveaxis(array.reshape(*before, size, -1, *after), dim, 0)


def sum_at_owner(array, axis, dim):
    size = lax.axis_size(axis)
    parts = lax.all_to_all(cut_along(array, dim, size), axis, 0, 0, tiled=True)
    return jnp.sum(parts.astype(jnp.float32), axis=0)


def by_axis(array, axes):
    for axis in axes:
        array = lax.psum(array, axis)
    return array


def sent_to_all(array, axis):
    copies = jnp.broadcast_to(array, (lax.axis_size(axis), *array.shape))
    return lax.all_to_all(copies, axis, split_axis=0, concat_axis=0, tiled=True)


def laid_out(parts, dim):
    lengths = list(parts.shape[1:])
    lengths[dim] *= parts.shape[0]
    return jnp.moveaxis(parts, 0, dim).reshape(lengths)


def gathered_copies(array, axis, dim):
    parts = sent_to_all(array, axis)
    return laid_out(parts, dim)


def reduced_to_own(parts, axes, sequence):
    lengths = [lax.axis_size(a) for a in axes]
    parts = parts.reshape(*lengths, *parts.shape[1:])
    parts = parts.transpose(*sequence, *range(len(axes), parts.ndim))
    parts = parts.reshape(-1, *parts.shape[len(axes) :])
    for k in sequence:
        parts = lax.psum_scatter(parts, axes[k], scatter_dimension=0, tiled=True)
    return parts[0]


def sum_by_axis_2(array, axes, sequence, dim):
    size = lax.axis_size(axes)
    return reduced_to_own(cut_along(array, dim, size), axes, sequence)


def stratum_weights(strata):
    quantile = (strata.astype(jnp.float32) + 0.5) / STRATA
    levels = math.sqrt(2.0) * lax.erf_inv(2.0 * quantile - 1.0)
    fraction = jax.nn.sigmoid(levels)
    weight = jnp.exp(-0.5 * levels * levels) / (
        math.sqrt(2.0 * math.pi) * fraction * (1.0 - fraction)
    )
    return (fraction, weight)


def modulate(clean, noise, modulation, fraction):
    features = clean.shape[-1]
    anchor = clean.astype(jnp.float32)
    drift_field = noise.astype(jnp.float32)
    mix_frac = fraction[:, None, None]
    noisy_field = (1.0 - mix_frac) * anchor + mix_frac * drift_field
    target = drift_field - anchor
    row_mean = jnp.mean(noisy_field, -1, keepdims=True)
    centred = noisy_field - row_mean
    variance = jnp.mean(centred * centred, -1, keepdims=True)
    normed = centred * lax.rsqrt(variance + 1e-06)
    shifts = modulation[:, None, :features]
    scales = modulation[:, None, features : 2 * features]
    modulated = (normed * (1.0 + scales) + shifts).astype(jnp.bfloat16)
    return (noisy_field, target, modulated, modulation[:, 2 * features :])


def gelu_tanh(values):
    return jax.nn.gelu(values, approximate=True)


def local(clean, noise, modulation, strata, up_weight, down_weight):
    samples_here, rows_per, features = clean.shape
    tokens_here = samples_here * rows_per
    fraction, weight = stratum_weights(strata)
    noisy_field, target, modulated, gate_values = modulate(clean, noise, modulation, fraction)
    flat_rows = modulated.reshape(tokens_here, features)
    flat_noisy = noisy_field.reshape(tokens_here, features)
    flat_target = target.reshape(tokens_here, features)
    local_total = jnp.sum(weight)
    preact = jnp.dot(flat_rows, up_weight, preferred_element_type=jnp.float32)
    hidden = gelu_tanh(preact).astype(jnp.bfloat16)
    partial_value = jnp.dot(hidden, down_weight, preferred_element_type=jnp.float32)
    share_rows = tokens_here // lax.axis_size(MP)
    first_row = lax.axis_index(MP) * share_rows
    sample_range = jnp.arange(samples_here, dtype=jnp.int32)
    owners = (first_row + jnp.arange(share_rows, dtype=jnp.int32)) // rows_per
    picker = (owners[:, None] == sample_range[None, :]).astype(jnp.float32)
    own_weight = jnp.dot(picker, weight, precision=lax.Precision.HIGHEST)
    output = sum_at_owner(partial_value.astype(jnp.bfloat16), MP, 0)
    gate_rows = jnp.dot(picker, gate_values, precision=lax.Precision.HIGHEST)
    noisy_share = lax.dynamic_slice_in_dim(flat_noisy, first_row, share_rows, 0)
    target_share = lax.dynamic_slice_in_dim(flat_target, first_row, share_rows, 0)
    errors = noisy_share + gate_rows * output - target_share
    own_squares = jnp.sum(errors * errors, 1)
    loss_local = jnp.sum(own_weight * own_squares) / (rows_per * features)
    leading = jnp.where(lax.axis_index(MP) == 0, local_total, jnp.float32(0.0))
    grand_total, loss_sum = (by_axis(leading, DP_MP), by_axis(loss_local, DP_MP))
    factor = loss_scale * 2.0 / (grand_total * rows_per * features)
    slopes = (factor * own_weight[:, None] * gate_rows * errors).astype(jnp.bfloat16)
    slopes = gathered_copies(slopes, MP, 0)
    hidden_slope = lax.dot_general(
        slopes, down_weight, (((1,), (1,)), ((), ())), preferred_element_type=jnp.float32
    )
    unused, pullback = jax.vjp(gelu_tanh, preact)
    pre_slope = pullback(hidden_slope)[0].astype(jnp.bfloat16)
    gradient = sum_by_axis_2(
        lax.dot_general(
            pre_slope, flat_rows, (((0,), (0,)), ((), ())), preferred_element_type=jnp.float32
        ),
        DP,
        (1, 0),
        0,
    )
    return (gradient, loss_sum / grand_total)


def solution(mesh):
    finer = Mesh(mesh.devices.reshape(12, 8, 4, 2), ("dp_0", "dp_1", "mp_0", "mp_1"))
    return jax.shard_map(
        local,
        mesh=finer,
        in_specs=(
            P(DP, None, None),
            P(DP, None, None),
            P(DP, None),
            P(DP),
            P(None, MP),
            P(MP, None),
        ),
        out_specs=(P(MP_DP, None), P()),
        check_vma=False,
    )
```

profile of v0, /device:TPU:4, one launch (start us, length us, event | category | flops | bytes accessed | tf_op | source)
XLA Modules:
  0.0 297.3 jit_solution(11336196759337821878)
XLA Ops:
  7.2 0.0 copy-start
  7.2 1.5 fusion.35
  8.7 0.8 slice_add_fusion
  9.4 4.3 %fusion.36 = (f32[2,128]{1,0:T(2,128)S(1)}, f32[2,128,2432]{2,1,0:T(8,128)S(1)}, f32[2,128,2432]{2,1,0:T(8,128)}) fusion(bf16[2,128,2432]{2,1,0:T(8,128)(2,1)} %param.7, f32[2]{0:T(128)S(1)} %get-tuple-element.14, bf16[2,128,2432]{2,1,0:T(8,128)(2,1)} %param.6, f32[2]{0:T(128)S(1)} %broadcast_subtract_fusion), kind=kLoop, calls=%fused_computation.69 | loop fusion | flops 4357888 | bytes 7472144 | tf_op jit(solution)/shard_map/reduce_sum | solution.py:84
  13.7 0.4 multiply_reduce_fusion
  14.1 0.0 copy-start.3
  14.1 0.6 add_convert_fusion
  14.8 0.4 copy-done.1
  15.2 1.8 copy-done.3
  17.0 1.1 fusion.38
  18.1 2.4 convolution_convert_fusion
  20.5 13.6 %all-to-all-start = ((bf16[8,32,2432]{2,1,0:T(8,128)(2,1)}), bf16[8,32,2432]{2,1,0:T(8,128)(2,1)}, u32[]{:S(2)}, u32[]{:S(2)}) async-start(bf16[8,32,2432]{2,1,0:T(8,128)(2,1)} %bitcast.48), calls=%async_computation | async-start | bytes 2490368 | tf_op jit(solution)/shard_map/all_to_all | solution.py:26
  34.8 14.3 %all-to-all-done = bf16[8,32,2432]{2,1,0:T(8,128)(2,1)} async-done(((bf16[8,32,2432]{2,1,0:T(8,128)(2,1)}), bf16[8,32,2432]{2,1,0:T(8,128)(2,1)}, u32[]{:S(2)}, u32[]{:S(2)}) %all-to-all-start) | async-done | bytes 1245216 | tf_op jit(solution)/shard_map/all_to_all | solution.py:26
  49.1 1.5 convert_reduce_fusion
  50.6 2.4 multiply_reduce_fusion.1
  53.0 0.8 multiply_reduce_fusion.2
  54.4 25.0 %all-reduce.1 = (f32[]{:T(128)}, f32[]{:T(128)}) all-reduce(f32[]{:T(128)S(6)} %select_n.17, f32[]{:T(128)S(6)} %div.43), channel_id=1, replica_groups=mesh['dp_0'=12,'dp_1'=8,'mp_0'=4,'mp_1'=2] {'dp_0'}, use_global_device_ids=true, to_apply=%region_1.0 | all-reduce | flops 2 | bytes 16 | tf_op jit(solution)/shard_map/psum | solution.py:32
  79.4 18.3 %all-reduce.2 = (f32[]{:T(128)}, f32[]{:T(128)}) all-reduce(f32[]{:T(128)} %get-tuple-element.2, f32[]{:T(128)} %get-tuple-element.3), channel_id=1, replica_groups=mesh['dp_0'=12,'dp_1'=8,'mp_0'=4,'mp_1'=2] {'dp_1'}, use_global_device_ids=true, to_apply=%region_2.0 | all-reduce | flops 2 | bytes 16 | tf_op jit(solution)/shard_map/psum | solution.py:32
  97.7 10.0 %all-reduce.3 = (f32[]{:T(128)}, f32[]{:T(128)}) all-reduce(f32[]{:T(128)} %get-tuple-element.4, f32[]{:T(128)} %get-tuple-element.5), channel_id=1, replica_groups=mesh['dp_0'=12,'dp_1'=8,'mp_0'=4,'mp_1'=2] {'mp_0'}, use_global_device_ids=true, to_apply=%region_3.4 | all-reduce | flops 2 | bytes 16 | tf_op jit(solution)/shard_map/psum | solution.py:32
  107.6 3.1 %all-reduce.4 = (f32[]{:T(128)}, f32[]{:T(128)}) all-reduce(f32[]{:T(128)} %get-tuple-element.6, f32[]{:T(128)} %get-tuple-element.7), channel_id=1, replica_groups=mesh['dp_0'=12,'dp_1'=8,'mp_0'=4,'mp_1'=2] {'mp_1'}, use_global_device_ids=true, to_apply=%region_4.5 | all-reduce | flops 2 | bytes 16 | tf_op jit(solution)/shard_map/psum | solution.py:32
  111.5 1.2 multiply_convert_fusion
  112.7 0.1 broadcast_in_dim.2
  112.8 20.4 %all_to_all.10 = bf16[8,32,2432]{2,1,0:T(8,128)(2,1)S(1)} all-to-all(bf16[8,32,2432]{2,1,0:T(8,128)(2,1)S(1)} %broadcast_in_dim.2), channel_id=1, replica_groups=mesh['dp_0'=12,'dp_1'=8,'mp_0'=4,'mp_1'=2] {'mp_0','mp_1'}, dimensions={0} | all-to-all | bytes 2490368 | tf_op jit(solution)/shard_map/all_to_all | solution.py:38
  133.1 2.1 fusion.7
  135.2 1.8 dot_general.31
  137.1 2.5 convolution_bitcast_fusion
  139.5 4.3 %copy.12 = f32[8,12,7,2432]{3,2,1,0:T(8,128)} copy(f32[8,12,7,2432]{3,0,2,1:T(8,128)S(1)} %convolution_bitcast_fusion) | data formatting | bytes 13074432 | tf_op jit(solution)/shard_map/transpose | solution.py:55
  143.9 0.0 reduce-scatter.5.cloned.1.call-update
  143.9 0.0 reduce-scatter.7.cloned.1.call-start
  143.9 83.6 %reduce-scatter.5.cloned.1.call-done = f32[12,7,2432]{2,1,0:T(8,128)} async-done(((f32[96,7,2432]{2,1,0:T(8,128)}), f32[12,7,2432]{2,1,0:T(8,128)}) %reduce-scatter.5.cloned.1.call-update) | async-done | bytes 817168 | tf_op jit(solution)/shard_map/reduce_scatter | solution.py:58
  227.6 0.0 reduce-scatter.7.cloned.1.call-update
  228.9 60.4 %reduce-scatter.7.cloned.1.call-done = f32[1,7,2432]{2,1,0:T(8,128)} async-done(((f32[12,7,2432]{2,1,0:T(8,128)}), f32[1,7,2432]{2,1,0:T(8,128)}) %reduce-scatter.7.cloned.1.call-update) | async-done | bytes 68112
  (14 shorter events, 0.0 us)
Async XLA Ops:
  7.2 10.9 %copy-start = (bf16[672,2432]{1,0:T(8,128)(2,1)S(1)}, bf16[672,2432]{1,0:T(8,128)(2,1)}, u32[]{:S(2)}) copy-start(bf16[672,2432]{1,0:T(8,128)(2,1)} %param.11) | copy-start | bytes 9805828
  13.7 1.5 copy-start.1
  14.1 2.9 copy-start.3
  15.2 2.9 copy-start.2
  18.1 2.4 copy-start.4
  20.5 28.6 %all-to-all-start = ((bf16[8,32,2432]{2,1,0:T(8,128)(2,1)}), bf16[8,32,2432]{2,1,0:T(8,128)(2,1)}, u32[]{:S(2)}, u32[]{:S(2)}) async-start(bf16[8,32,2432]{2,1,0:T(8,128)(2,1)} %bitcast.48), calls=%async_computation | async-start | bytes 2490368 | tf_op jit(solution)/shard_map/all_to_all | solution.py:26
  34.1 193.5 %reduce-scatter.5.cloned.1.call-start = ((), (), s32[]{:S(2)}) async-start(), calls=%async_computation.4 | async-start | bytes 8404992 | tf_op jit(solution)/shard_map/reduce_scatter | solution.py:58
  111.4 21.7 %copy-start.5 = (f32[256,672]{0,1:T(8,128)S(1)}, f32[256,672]{0,1:T(8,128)}, u32[]{:S(2)}) copy-start(f32[256,672]{0,1:T(8,128)} %copy-done.4) | copy-start | bytes 2064388
  143.9 145.4 %reduce-scatter.7.cloned.1.call-start = ((), (), s32[]{:S(2)}) async-start(), calls=%async_computation.5 | async-start | bytes 1011712
Sparse Core Ops, SparseCore 0:
  144.0 83.5 reduce-scatter.4
  231.3 58.0 reduce-scatter.6
where the time goes:
time: 298 us; the launch traced here: 297 us
  waiting for transfers between devices  158 us (53%)
  blocking collectives  76.7 us (26%)
  between operations  18.6 us (6%)
  starting transfers between devices  13.7 us (5%)
  matrix products  11.2 us (4%)
  other arithmetic  10.3 us (3%)
  local copies, waits for them, and re-layouts  8.45 us (3%)
    reduce_scatter x1, waiting for transfers between devices, reduced_to_own(): parts = lax.psum_scatter(parts, axes[k], scatter_dimension=0, tiled=True)  83.6 us
    unnamed x3, waiting for transfers between devices  60.5 us
    psum x4, blocking collectives, by_axis(): array = lax.psum(array, axis)  56.3 us
    all_to_all x1, blocking collectives, sent_to_all(): return lax.all_to_all(copies, axis, split_axis=0, concat_axis=0, tiled=True)  20.4 us
    all_to_all x1, waiting for transfers between devices, sum_at_owner(): parts = lax.all_to_all(cut_along(array, dim, size), axis, 0, 0, tiled=True)  14.3 us
    all_to_all x1, starting transfers between devices, sum_at_owner(): parts = lax.all_to_all(cut_along(array, dim, size), axis, 0, 0, tiled=True)  13.6 us
  transfers between devices with their start and end apart: 3, of which 3 were waited for; matrix products, arithmetic and copies ran while one was open for 0% of the time, Pallas kernels for 0%

commit v1 on v0

v1 whole, which is shorter than its diff:
```python
import math

import jax
import jax.numpy as jnp
from jax import lax
from jax.sharding import Mesh
from jax.sharding import PartitionSpec as P

STRATA = 64
DP = ("z", "y")
MP = ("x", "c")
MP_DP = ("x", "c", "z", "y")

loss_scale = 1048576.0


def stratum_weights(strata):
    quantile = (strata.astype(jnp.float32) + 0.5) / STRATA
    levels = math.sqrt(2.0) * lax.erf_inv(2.0 * quantile - 1.0)
    fraction = jax.nn.sigmoid(levels)
    weight = jnp.exp(-0.5 * levels * levels) / (
        math.sqrt(2.0 * math.pi) * fraction * (1.0 - fraction)
    )
    return (fraction, weight)


def blend(clean, noise, fraction):
    anchor = clean.astype(jnp.float32)
    drift_field = noise.astype(jnp.float32)
    noisy_field = (1.0 - fraction) * anchor + fraction * drift_field
    return (noisy_field, drift_field - anchor)


def gelu_tanh(values):
    return jax.nn.gelu(values, approximate=True)


def swap_cores(array):
    return lax.ppermute(array, "c", [(0, 1), (1, 0)])


def exchanged(array, axis):
    return lax.all_to_all(array, axis, 0, 0, tiled=True)


def coded(values):
    first = lax.reduce_precision(values, 8, 7)
    second = lax.reduce_precision(values - first, 8, 7)
    third = (values - first) - second
    return jnp.stack([first, second, third], -1).reshape(-1).astype(jnp.bfloat16)


def decoded(pieces):
    pieces = pieces.astype(jnp.float32)
    return jnp.sum(pieces.reshape(-1, pieces.shape[-1] // 3, 3), axis=(0, 2))


def lane_row(values, lanes):
    return jnp.pad(values, (0, lanes - values.shape[0]))


def with_totals(block, totals):
    row = lane_row(coded(totals), block.shape[-1])
    place = lax.broadcasted_iota(jnp.int32, block.shape, 1)
    return jnp.where(place == block.shape[1] - 1, row, block.astype(jnp.bfloat16))


def local(clean, noise, modulation, strata, up_weight, down_weight):
    samples_here, rows_per, features = clean.shape
    size_x, size_y, size_z = (lax.axis_size(a) for a in ("x", "y", "z"))
    units = up_weight.shape[1]
    share = rows_per // size_x
    core = lax.axis_index("c")
    other_up = swap_cores(up_weight)
    other_down = swap_cores(down_weight)

    def own(array):
        return lax.dynamic_index_in_dim(array, core, 0, keepdims=False)

    fraction, weight = stratum_weights(own(strata))
    latent, drift, conditioning = own(clean), own(noise), own(modulation)
    shift = conditioning[:features]
    scale = conditioning[features : 2 * features]
    gate = conditioning[2 * features :]
    noisy_field, _ = blend(latent, drift, fraction)
    row_mean = jnp.mean(noisy_field, -1, keepdims=True)
    centred = noisy_field - row_mean
    variance = jnp.mean(centred * centred, -1, keepdims=True)
    normed = centred * lax.rsqrt(variance + 1e-06)
    modulated = (normed * (1.0 + scale) + shift).astype(jnp.bfloat16)
    gathered = lax.all_gather(modulated, "y", axis=0, tiled=False)

    ups, downs = (up_weight, other_up), (down_weight, other_down)
    preacts = [jnp.dot(modulated, w, preferred_element_type=jnp.float32) for w in ups]
    partial_value = sum(
        jnp.dot(gelu_tanh(p).astype(jnp.bfloat16), w, preferred_element_type=jnp.float32)
        for p, w in zip(preacts, downs)
    )
    parts = exchanged(partial_value.astype(jnp.bfloat16).reshape(size_x, share, features), "x")
    output = jnp.sum(parts.astype(jnp.float32), axis=0)

    first_row = lax.axis_index("x") * share
    rows = [lax.dynamic_slice_in_dim(a, first_row, share, 0) for a in (latent, drift)]
    noisy_share, target_share = blend(*rows, fraction)
    errors = noisy_share + gate * output - target_share
    loss_local = weight * jnp.sum(errors * errors) / (rows_per * features)
    coefficient = (loss_scale * 2.0 / (rows_per * features)) * weight
    slopes = (coefficient * gate * errors).astype(jnp.bfloat16)
    side = jnp.broadcast_to(lane_row(coded(loss_local), 128), (share, 128))
    message = jnp.concatenate([slopes, side], 1)
    message = exchanged(jnp.broadcast_to(message, (size_x, *message.shape)), "x")
    loss_here = decoded(message[:, 0, features : features + 3])
    slopes = message[:, :, :features].reshape(rows_per, features)

    pre_slopes = []
    for p, w in zip(preacts, downs):
        hidden_slope = lax.dot_general(
            w, slopes, (((1,), (1,)), ((), ())), preferred_element_type=jnp.float32
        )
        unused, pullback = jax.vjp(gelu_tanh, p.T)
        pre_slopes.append(pullback(hidden_slope)[0].astype(jnp.bfloat16))
    group = units // (size_z * size_y)
    pre_slope = jnp.stack(pre_slopes).reshape(2, size_z, size_y, group, rows_per)
    totals = jnp.concatenate([loss_here, weight[None]])
    extra = jnp.broadcast_to(
        lane_row(coded(totals), rows_per), (2, size_z, size_y, 1, rows_per)
    )
    pre_slope = jnp.concatenate([pre_slope, extra], 3).transpose(2, 0, 1, 3, 4)
    pre_slope = exchanged(pre_slope.reshape(size_y, -1, rows_per), "y")
    totals = decoded(pre_slope[:, group, :6])
    gradient = lax.dot_general(
        pre_slope, gathered, (((0, 2), (0, 1)), ((), ())), preferred_element_type=jnp.float32
    ).reshape(2, size_z, group + 1, features)
    received = swap_cores(with_totals(gradient[1], totals))
    totals = totals + decoded(received[0, group, :6])
    gradient = gradient[0] + received.astype(jnp.float32)
    parts = exchanged(with_totals(gradient, totals), "z")
    totals = decoded(parts[:, group, :6])
    gradient = jnp.sum(parts.astype(jnp.float32), axis=0)[:group]
    return (gradient / totals[1], totals[0] / totals[1])


def solution(mesh):
    finer = Mesh(mesh.devices.reshape(12, 8, 4, 2), ("z", "y", "x", "c"))
    return jax.shard_map(
        local,
        mesh=finer,
        in_specs=(
            P(DP, None, None),
            P(DP, None, None),
            P(DP, None),
            P(DP),
            P(None, MP),
            P(MP, None),
        ),
        out_specs=(P(MP_DP, None), P()),
        check_vma=False,
    )
```

time: 298 us -> 154 us (0.52)
  the two profiles are of different devices: /device:TPU:4 before, /device:TPU:2 now
where the time goes in v1:
time: 154 us; the launch traced here: 153 us
  blocking collectives  46.3 us (30%)
  waiting for transfers between devices  28.2 us (18%)
  starting transfers between devices  22.7 us (15%)
  between operations  22.2 us (14%)
  matrix products  15.4 us (10%)
  other arithmetic  10.1 us (7%)
  local copies, waits for them, and re-layouts  8.24 us (5%)
    all_to_all x2, blocking collectives, exchanged(): return lax.all_to_all(array, axis, 0, 0, tiled=True)  46.3 us
    all_to_all x2, waiting for transfers between devices, exchanged(): return lax.all_to_all(array, axis, 0, 0, tiled=True)  23.2 us
    all_to_all x2, starting transfers between devices, exchanged(): return lax.all_to_all(array, axis, 0, 0, tiled=True)  16.4 us
    ppermute x3, starting transfers between devices, swap_cores(): return lax.ppermute(array, 'c', [(0, 1), (1, 0)])  6.25 us
    ppermute x3, waiting for transfers between devices, swap_cores(): return lax.ppermute(array, 'c', [(0, 1), (1, 0)])  4.93 us
    dot_general x2, matrix products, local(): lax.dot_general(w, slopes, (((1,), (1,)), ((), ())), preferred_element_ty...  4.79 us
    dot_general x2, matrix products, local(): jnp.dot(modulated, w, preferred_element_type=jnp.float32)  4.31 us
    dot_general x1, matrix products, local(): lax.dot_general(pre_slope, gathered, (((0, 2), (0, 1)), ((), ())), prefer...  3.61 us
  transfers between devices with their start and end apart: 6, of which 4 were waited for; matrix products, arithmetic and copies ran while one was open for 13% of the time, Pallas kernels for 0%

profile of v1, /device:TPU:2, one launch (start us, length us, event | category | flops | bytes accessed | tf_op | source)
XLA Modules:
  0.0 153.2 jit_solution(2571670149991379983)
XLA Ops:
  7.2 1.3 dynamic_slice.21
  9.4 1.7 %fusion.56 = f32[128]{0:T(128)S(1)} fusion(bf16[2,128,2432]{2,1,0:T(8,128)(2,1)} %param.7, s32[]{:T(128)S(6)} %select_n.24, f32[]{:T(128)S(6)} %div.25, bf16[2,128,2432]{2,1,0:T(8,128)(2,1)} %param.6, f32[]{:T(128)S(6)} %sub.122), kind=kLoop, calls=%fused_computation.82 | loop fusion | flops 1867648 | bytes 1245708 | tf_op jit(solution)/shard_map/reduce_sum | solution.py:86
  11.2 1.5 multiply_reduce_fusion
  12.9 1.3 add_convert_fusion
  14.3 1.9 %collective-permute-start = (bf16[2432,672]{0,1:T(8,128)(2,1)}, bf16[2432,672]{0,1:T(8,128)(2,1)S(1)}, u32[]{:S(2)}, u32[]{:S(2)}) collective-permute-start(bf16[2432,672]{0,1:T(8,128)(2,1)} %param.10), channel_id=1, source_target_pairs={{0,1},{1,0},{2,3},{3,2},{4,5},{5,4},{6,7},{7,6},{8,9},{9,8},{10,11... | collective-permute-start | bytes 9805832 | tf_op jit(solution)/shard_map/ppermute | solution.py:39
  16.2 2.4 %collective-permute-start.1 = (bf16[672,2432]{1,0:T(8,128)(2,1)}, bf16[672,2432]{1,0:T(8,128)(2,1)S(1)}, u32[]{:S(2)}, u32[]{:S(2)}) collective-permute-start(bf16[672,2432]{1,0:T(8,128)(2,1)} %param.11), channel_id=1, source_target_pairs={{0,1},{1,0},{2,3},{3,2},{4,5},{5,4},{6,7},{7,6},{8,9},{9,8},{10,11... | collective-permute-start | bytes 9805832 | tf_op jit(solution)/shard_map/ppermute | solution.py:39
  18.7 3.2 %fusion.73 = f32[128,672]{0,1:T(8,128)S(1)} fusion(bf16[2432,672]{0,1:T(8,128)(2,1)} %param.10, f32[2432]{0:T(1024)S(1)} %get-tuple-element.5, f32[2432]{0:T(1024)S(1)} %get-tuple-element.3, f32[128]{0:T(128)S(1)} %add_rsqrt_fusion, f32[128]{0:T(128)S(1)} %broadcast_multiply_fusion, bf16[2,128,2432]{2,1,0:T(8,128)(2,1)S(1)} %copy-done, s32[]{:T(128)S(6)} %select_n.24, ...), kind=kOutput, calls=%fused_computation.131 | convolution fusion | flops 421494784 | bytes 4883468 | tf_op jit(solution)/shard_map/dot_general | solution.py:94
  21.9 0.7 fusion.46
  22.6 1.1 fusion.72
  23.8 3.1 %collective-permute-done.1 = bf16[672,2432]{1,0:T(8,128)(2,1)S(1)} collective-permute-done((bf16[672,2432]{1,0:T(8,128)(2,1)}, bf16[672,2432]{1,0:T(8,128)(2,1)S(1)}, u32[]{:S(2)}, u32[]{:S(2)}) %collective-permute-start.1) | collective-permute-done | bytes 3268640 | tf_op jit(solution)/shard_map/ppermute | solution.py:39
  26.9 1.9 %fusion = bf16[128,2432]{1,0:T(8,128)(2,1)} fusion(f32[128,2432]{1,0:T(8,128)S(1)} %fusion.46, bf16[672,2432]{1,0:T(8,128)(2,1)S(1)} %collective-permute-done.1, f32[128,672]{0,1:T(8,128)S(1)} %fusion.72), kind=kOutput, calls=%fused_computation.2 | convolution fusion | flops 419778560 | bytes 5480448 | tf_op jit(solution)/shard_map/dot_general | solution.py:96
  28.9 13.0 %all-to-all-start = ((bf16[4,32,2432]{2,1,0:T(8,128)(2,1)}), bf16[4,32,2432]{2,1,0:T(8,128)(2,1)S(1)}, u32[]{:S(2)}, u32[]{:S(2)}) async-start(bf16[4,32,2432]{2,1,0:T(8,128)(2,1)} %bitcast.107), calls=%async_computation | async-start | bytes 1245184 | tf_op jit(solution)/shard_map/all_to_all | solution.py:43
  41.8 9.7 %all-to-all-done = bf16[4,32,2432]{2,1,0:T(8,128)(2,1)S(1)} async-done(((bf16[4,32,2432]{2,1,0:T(8,128)(2,1)}), bf16[4,32,2432]{2,1,0:T(8,128)(2,1)S(1)}, u32[]{:S(2)}, u32[]{:S(2)}) %all-to-all-start) | async-done | bytes 622624 | tf_op jit(solution)/shard_map/all_to_all | solution.py:43
  51.6 0.8 multiply_reduce_fusion.1
  57.0 13.3 %all_to_all.20 = bf16[4,32,2560]{2,1,0:T(8,128)(2,1)S(1)} all-to-all(bf16[4,32,2560]{2,1,0:T(8,128)(2,1)S(1)} %broadcast_in_dim.24), channel_id=1, replica_groups=mesh['z'=12,'y'=8,'x'=4,'c'=2] {'x'}, dimensions={0} | all-to-all | bytes 1310720 | tf_op jit(solution)/shard_map/all_to_all | solution.py:43
  70.4 0.8 copy-done.6
  71.2 0.8 copy-done.7
  72.1 1.8 %fusion.12 = bf16[672,128]{1,0:T(8,128)(2,1)} fusion(f32[128,672]{0,1:T(8,128)S(1)} %copy-done.9, bf16[128,2432]{1,0:T(8,128)(2,1)S(1)} %bitcast.108, bf16[672,2432]{1,0:T(8,128)(2,1)S(1)} %copy-done.3), kind=kOutput, calls=%fused_computation.35 | convolution fusion | flops 420102144 | bytes 4407296 | tf_op jit(solution)/shard_map/dot_general | solution.py:117
  73.9 1.0 stack.50
  74.9 3.0 %fusion.19 = bf16[672,128]{1,0:T(8,128)(2,1)} fusion(f32[128,672]{0,1:T(8,128)} %copy-done.10, bf16[128,2432]{1,0:T(8,128)(2,1)} %bitcast.109, bf16[672,2432]{1,0:T(8,128)(2,1)S(1)} %copy-done.5), kind=kOutput, calls=%fused_computation.42 | convolution fusion | flops 420102144 | bytes 4407296 | tf_op jit(solution)/shard_map/dot_general | solution.py:117
  77.8 1.0 stack.51
  78.8 0.7 slice.60
  80.9 0.7 reduce-precision_convert_fusion
  82.0 0.8 copy.31
  82.9 3.5 %all-to-all-start.2 = ((bf16[8,192,128]{2,1,0:T(8,128)(2,1)}), bf16[8,192,128]{2,1,0:T(8,128)(2,1)S(1)}, u32[]{:S(2)}, u32[]{:S(2)}) async-start(bf16[8,192,128]{2,1,0:T(8,128)(2,1)} %bitcast.16), calls=%async_computation.2 | async-start | bytes 786432 | tf_op jit(solution)/shard_map/all_to_all | solution.py:43
  86.3 13.6 %all-to-all-done.2 = bf16[8,192,128]{2,1,0:T(8,128)(2,1)S(1)} async-done(((bf16[8,192,128]{2,1,0:T(8,128)(2,1)}), bf16[8,192,128]{2,1,0:T(8,128)(2,1)S(1)}, u32[]{:S(2)}, u32[]{:S(2)}) %all-to-all-start.2) | async-done | bytes 393248 | tf_op jit(solution)/shard_map/all_to_all | solution.py:43
  100.4 3.6 %convolution_bitcast_fusion = f32[192,2432]{1,0:T(8,128)S(1)} fusion(bf16[8,192,128]{2,1,0:T(8,128)(2,1)S(1)} %all-to-all-done.2, bf16[8,128,2432]{2,1,0:T(8,128)(2,1)} %all-gather.2.cloned.1.call-done), kind=kOutput, calls=%fused_computation | convolution fusion | flops 956301312 | bytes 7241728 | tf_op jit(solution)/shard_map/dot_general | solution.py:131
  104.2 1.9 %collective-permute-start.2 = (bf16[12,8,2432]{2,1,0:T(8,128)(2,1)S(1)}, bf16[12,8,2432]{2,1,0:T(8,128)(2,1)S(1)}, u32[]{:S(2)}, u32[]{:S(2)}) collective-permute-start(bf16[12,8,2432]{2,1,0:T(8,128)(2,1)S(1)} %fusion.4), channel_id=1, source_target_pairs={{0,1},{1,0},{2,3},{3,2},{4,5},{5,4},{6,7},{7,6},{8,9},{9,8},{10,11... | collective-permute-start | bytes 1400840 | tf_op jit(solution)/shard_map/ppermute | solution.py:39
  106.1 1.8 %collective-permute-done.2 = bf16[12,8,2432]{2,1,0:T(8,128)(2,1)S(1)} collective-permute-done((bf16[12,8,2432]{2,1,0:T(8,128)(2,1)S(1)}, bf16[12,8,2432]{2,1,0:T(8,128)(2,1)S(1)}, u32[]{:S(2)}, u32[]{:S(2)}) %collective-permute-start.2) | collective-permute-done | bytes 466976 | tf_op jit(solution)/shard_map/ppermute | solution.py:39
  108.5 33.0 %all_to_all.21 = bf16[12,8,2432]{2,1,0:T(8,128)(2,1)S(1)} all-to-all(bf16[12,8,2432]{2,1,0:T(8,128)(2,1)S(1)} %fusion.5), channel_id=1, replica_groups=mesh['z'=12,'y'=8,'x'=4,'c'=2] {'z'}, dimensions={0} | all-to-all | bytes 933888 | tf_op jit(solution)/shard_map/all_to_all | solution.py:43
  141.8 0.7 fusion.74
  143.9 1.3 slice_divide_fusion
  (67 shorter events, 3.9 us)
Async XLA Ops:
  7.2 4.0 %copy-start = (bf16[2,128,2432]{2,1,0:T(8,128)(2,1)S(1)}, bf16[2,128,2432]{2,1,0:T(8,128)(2,1)}, u32[]{:S(2)}) copy-start(bf16[2,128,2432]{2,1,0:T(8,128)(2,1)} %param.7) | copy-start | bytes 3735556
  7.2 93.2 %all-gather.2.cloned.1.call-start = ((), (), s32[]{:S(2)}) async-start(), calls=%async_computation.4 | async-start | bytes 5603328 | tf_op jit(solution)/shard_map/all_gather | solution.py:91
  9.4 3.3 %copy-start.11 = (f32[2,7296]{1,0:T(2,128)S(1)}, f32[2,7296]{1,0:T(2,128)}, u32[]{:S(2)}) copy-start(f32[2,7296]{1,0:T(2,128)} %param.8) | copy-start | bytes 175108
  9.4 3.5 %copy-start.1 = (bf16[2,128,2432]{2,1,0:T(8,128)(2,1)S(1)}, bf16[2,128,2432]{2,1,0:T(8,128)(2,1)}, u32[]{:S(2)}) copy-start(bf16[2,128,2432]{2,1,0:T(8,128)(2,1)} %param.6) | copy-start | bytes 3735556
  14.3 8.3 %collective-permute-start = (bf16[2432,672]{0,1:T(8,128)(2,1)}, bf16[2432,672]{0,1:T(8,128)(2,1)S(1)}, u32[]{:S(2)}, u32[]{:S(2)}) collective-permute-start(bf16[2432,672]{0,1:T(8,128)(2,1)} %param.10), channel_id=1, source_target_pairs={{0,1},{1,0},{2,3},{3,2},{4,5},{5,4},{6,7},{7,6},{8,9},{9,8},{10,11... | collective-permute-start | bytes 9805832 | tf_op jit(solution)/shard_map/ppermute | solution.py:39
  16.2 10.7 %collective-permute-start.1 = (bf16[672,2432]{1,0:T(8,128)(2,1)}, bf16[672,2432]{1,0:T(8,128)(2,1)S(1)}, u32[]{:S(2)}, u32[]{:S(2)}) collective-permute-start(bf16[672,2432]{1,0:T(8,128)(2,1)} %param.11), channel_id=1, source_target_pairs={{0,1},{1,0},{2,3},{3,2},{4,5},{5,4},{6,7},{7,6},{8,9},{9,8},{10,11... | collective-permute-start | bytes 9805832 | tf_op jit(solution)/shard_map/ppermute | solution.py:39
  18.6 3.2 %copy-start.2 = (bf16[672,2432]{1,0:T(8,128)(2,1)S(1)}, bf16[672,2432]{1,0:T(8,128)(2,1)}, u32[]{:S(2)}) copy-start(bf16[672,2432]{1,0:T(8,128)(2,1)} %param.11) | copy-start | bytes 9805828
  21.9 0.8 copy-start.8
  23.8 5.1 %copy-start.10 = (f32[128,672]{0,1:T(8,128)}, f32[128,672]{0,1:T(8,128)S(1)}, u32[]{:S(2)}) copy-start(f32[128,672]{0,1:T(8,128)S(1)} %fusion.72) | copy-start | bytes 1032196
  26.9 1.9 %copy-start.4 = (bf16[672,2432]{1,0:T(8,128)(2,1)}, bf16[672,2432]{1,0:T(8,128)(2,1)S(1)}, u32[]{:S(2)}) copy-start(bf16[672,2432]{1,0:T(8,128)(2,1)S(1)} %collective-permute-done.1) | copy-start | bytes 9805828
  28.9 22.6 %all-to-all-start = ((bf16[4,32,2432]{2,1,0:T(8,128)(2,1)}), bf16[4,32,2432]{2,1,0:T(8,128)(2,1)S(1)}, u32[]{:S(2)}, u32[]{:S(2)}) async-start(bf16[4,32,2432]{2,1,0:T(8,128)(2,1)} %bitcast.107), calls=%async_computation | async-start | bytes 1245184 | tf_op jit(solution)/shard_map/all_to_all | solution.py:43
  56.9 15.1 %copy-start.9 = (f32[128,672]{0,1:T(8,128)S(1)}, f32[128,672]{0,1:T(8,128)}, u32[]{:S(2)}) copy-start(f32[128,672]{0,1:T(8,128)} %copy-done.8) | copy-start | bytes 1032196
  57.0 15.1 %copy-start.3 = (bf16[672,2432]{1,0:T(8,128)(2,1)S(1)}, bf16[672,2432]{1,0:T(8,128)(2,1)}, u32[]{:S(2)}) copy-start(bf16[672,2432]{1,0:T(8,128)(2,1)} %param.11) | copy-start | bytes 9805828
  70.3 0.9 copy-start.6
  71.2 0.8 copy-start.7
  72.0 2.8 %copy-start.5 = (bf16[672,2432]{1,0:T(8,128)(2,1)S(1)}, bf16[672,2432]{1,0:T(8,128)(2,1)}, u32[]{:S(2)}) copy-start(bf16[672,2432]{1,0:T(8,128)(2,1)} %copy-done.4) | copy-start | bytes 9805828
  82.9 17.1 %all-to-all-start.2 = ((bf16[8,192,128]{2,1,0:T(8,128)(2,1)}), bf16[8,192,128]{2,1,0:T(8,128)(2,1)S(1)}, u32[]{:S(2)}, u32[]{:S(2)}) async-start(bf16[8,192,128]{2,1,0:T(8,128)(2,1)} %bitcast.16), calls=%async_computation.2 | async-start | bytes 786432 | tf_op jit(solution)/shard_map/all_to_all | solution.py:43
  104.2 3.7 %collective-permute-start.2 = (bf16[12,8,2432]{2,1,0:T(8,128)(2,1)S(1)}, bf16[12,8,2432]{2,1,0:T(8,128)(2,1)S(1)}, u32[]{:S(2)}, u32[]{:S(2)}) collective-permute-start(bf16[12,8,2432]{2,1,0:T(8,128)(2,1)S(1)} %fusion.4), channel_id=1, source_target_pairs={{0,1},{1,0},{2,3},{3,2},{4,5},{5,4},{6,7},{7,6},{8,9},{9,8},{10,11... | collective-permute-start | bytes 1400840 | tf_op jit(solution)/shard_map/ppermute | solution.py:39
Sparse Core Ops, SparseCore 0:
  14.4 73.8 all-gather.1

commit v2 on v1

v2 whole, which is shorter than its diff:
```python
import functools
import math

import jax
import jax.numpy as jnp
from jax import lax
from jax.experimental import pallas as pl
from jax.experimental.pallas import tpu as pltpu
from jax.sharding import Mesh
from jax.sharding import PartitionSpec as P


STRATA = 64
DP = ("zb", "zi", "yb", "yi")
MP = ("x", "c")
MP_DP = (*MP, *DP)
LANES = 128
GROUP = 8
VMEM = 56 * 2**20

loss_scale = 1048576.0
f32 = jnp.float32
bf16 = jnp.bfloat16


def swap_cores(array):
    return lax.ppermute(array, "c", [(0, 1), (1, 0)])


def exchanged(array, axis):
    return lax.all_to_all(array, axis, 0, 0, tiled=True)


def gelu_tanh(values):
    return jax.nn.gelu(values, approximate=True)


def gelu_slope(values):
    root = math.sqrt(2.0 / math.pi)
    squares = values * values
    bend = jnp.tanh(root * (values + 0.044715 * squares * values))
    inner = root * (1.0 + (3.0 * 0.044715) * squares)
    return 0.5 * (1.0 + bend) + 0.5 * values * (1.0 - bend * bend) * inner


def erf_inverse(x):
    w = -jnp.log1p(-x * x)
    near = (2.81022636e-08, 3.43273939e-07, -3.5233877e-06, -4.39150654e-06, 0.00021858087,
            -0.00125372503, -0.00417768164, 0.246640727, 1.50140941)
    far = (-0.000200214257, 0.000100950558, 0.00134934322, -0.00367342844, 0.00573950773,
           -0.0076224613, 0.00943887047, 1.00167406, 2.83297682)
    small = w < 5.0
    w = jnp.where(small, w - 2.5, jnp.sqrt(w) - 3.0)
    p = jnp.where(small, near[0], far[0])
    for a, b in zip(near[1:], far[1:]):
        p = jnp.where(small, a, b) + p * w
    return p * x


def coded_row(values):
    lane = lax.broadcasted_iota(jnp.int32, (1, LANES), 1)
    row = jnp.zeros((1, LANES), f32)
    for k, value in enumerate(values):
        first = value.astype(bf16).astype(f32)
        second = (value - first).astype(bf16).astype(f32)
        third = (value - first) - second
        for j, piece in enumerate((first, second, third)):
            row = jnp.where(lane == 3 * k + j, piece, row)
    return row


def decoded(row, k):
    lane = lax.broadcasted_iota(jnp.int32, (1, LANES), 1)
    mine = (lane >= 3 * k) & (lane < 3 * k + 3)
    return jnp.sum(jnp.where(mine, row, 0.0), axis=1, keepdims=True)


def marked(block, row):
    place = lax.broadcasted_iota(jnp.int32, block.shape, 0) % GROUP
    return jnp.where(place == GROUP - 1, row, block)


def blend(clean, noise, fraction):
    anchor = clean.astype(f32)
    drift_field = noise.astype(f32)
    noisy_field = (1.0 - fraction) * anchor + fraction * drift_field
    return (noisy_field, drift_field - anchor)


def modulate_kernel(place, strata, clean, noise, modulation, modulated, info):
    features = clean.shape[-1]
    core = place[0]
    stratum = jnp.full((GROUP, LANES), strata[core].astype(f32), f32)
    level = math.sqrt(2.0) * erf_inverse(2.0 * ((stratum + 0.5) / STRATA) - 1.0)
    fraction = 1.0 / (1.0 + jnp.exp(-level))
    weight = jnp.exp(-0.5 * level * level) / (
        math.sqrt(2.0 * math.pi) * fraction * (1.0 - fraction)
    )
    info[0] = fraction
    info[1] = weight
    noisy_field, _ = blend(clean[0], noise[0], fraction[:1, :1])
    row_mean = jnp.mean(noisy_field, -1, keepdims=True)
    centred = noisy_field - row_mean
    variance = jnp.mean(centred * centred, -1, keepdims=True)
    normed = centred * lax.rsqrt(variance + 1e-06)
    shift = modulation[pl.ds(core, 1), :features]
    scale = modulation[pl.ds(core, 1), features : 2 * features]
    modulated[...] = (normed * (1.0 + scale) + shift).astype(bf16)


def loss_kernel(place, parts, clean, noise, modulation, info, message):
    copies, share, features = parts.shape
    fraction, weight = info[0][:1, :1], info[1][:1, :1]
    gate = modulation[pl.ds(place[0], 1), 2 * features :]
    output = parts[0].astype(f32)
    for j in range(1, copies):
        output = output + parts[j].astype(f32)
    noisy_share, target_share = blend(clean[0], noise[0], fraction)
    errors = noisy_share + gate * output - target_share
    squares = jnp.sum(jnp.sum(errors * errors, axis=0, keepdims=True), axis=1, keepdims=True)
    rows = clean.shape[1] * copies
    loss_local = weight * squares / (rows * features)
    coefficient = (loss_scale * 2.0 / (rows * features)) * weight
    slopes = (coefficient * gate * errors).astype(bf16)
    side = jnp.broadcast_to(coded_row([loss_local]), (share, LANES)).astype(bf16)
    for j in range(copies):
        message[j, :, :features] = slopes
        message[j, :, features:] = side


def backward_kernel(sizes, message, down_0, down_1, pre_0, pre_1, info, out, flat):
    outer_z, inner_z, outer_y, inner_y = sizes
    copies, share, width = message.shape
    features = width - LANES
    units = pre_0.shape[0]
    group = units // math.prod(sizes)
    slopes = message[:, :, :features].reshape(copies * share, features)
    for r, (down, pre) in enumerate(((down_0, pre_0), (down_1, pre_1))):
        hidden_slope = lax.dot_general(
            down[...], slopes, (((1,), (1,)), ((), ())), preferred_element_type=f32
        )
        flat[r * units : (r + 1) * units, :] = gelu_slope(pre[...]) * hidden_slope
    flat[2 * units :, :] = jnp.zeros((GROUP, LANES), f32)
    row = message[0, :1, features:].astype(f32)
    for j in range(1, copies):
        row = row + message[j, :1, features:].astype(f32)
    scalars = coded_row([decoded(row, 0), info[1][:1, :1]])
    for piece in range(inner_z * inner_y):
        zi, yi = divmod(piece, inner_y)
        for at in range(0, 2 * outer_z * outer_y, 2):
            halves = []
            for k in (at, at + 1):
                r, owner = divmod(k, outer_z * outer_y)
                zb, yb = divmod(owner, outer_y)
                owner = ((zb * inner_z + zi) * outer_y + yb) * inner_y + yi
                start = r * units + owner * group
                halves.append(flat[start : start + GROUP, :])
            block = marked(jnp.concatenate(halves, 0), scalars)
            out[piece, at * GROUP : (at + 2) * GROUP, :] = block.astype(bf16)


def gathered_product(place, pre_slope, blocks, first, size):
    columns = [pre_slope[place[2] ^ k, first : first + size, :] for k in range(len(blocks))]
    rows = [block[...] for block in blocks]
    return lax.dot_general(
        jnp.concatenate(columns, 1),
        jnp.concatenate(rows, 0),
        (((1,), (0,)), ((), ())),
        preferred_element_type=f32,
    )


def gathered_sums(pre_slope):
    row = pre_slope[0, :GROUP, :].astype(f32)[GROUP - 1 :, :]
    for k in range(1, pre_slope.shape[0]):
        row = row + pre_slope[k, :GROUP, :].astype(f32)[GROUP - 1 :, :]
    return [decoded(row, k) for k in range(2)]


def store_marked(out, block, sums):
    out[:, LANES:] = block[:, LANES:].astype(bf16)
    out[:, :LANES] = marked(block[:, :LANES], coded_row(sums)).astype(bf16)


def away_kernel(place, pre_slope, *refs):
    *blocks, out = refs
    half = out.shape[0]
    product = gathered_product(place, pre_slope, blocks, half, half)
    store_marked(out, product, gathered_sums(pre_slope))


def home_kernel(place, pre_slope, got, *refs):
    *blocks, out = refs
    half = out.shape[0]
    product = gathered_product(place, pre_slope, blocks, 0, half)
    got_row = got[:GROUP, :LANES].astype(f32)[GROUP - 1 :, :]
    sums = [a + decoded(got_row, k) for k, a in enumerate(gathered_sums(pre_slope))]
    store_marked(out, product + got[...].astype(f32), sums)


def finish_kernel(parts, gradient, loss):
    total = parts[0].astype(f32)
    for j in range(1, parts.shape[0]):
        total = total + parts[j].astype(f32)
    row = total[GROUP - 1 :, :LANES]
    loss_sum, weight_sum = decoded(row, 0), decoded(row, 1)
    gradient[...] = total[: GROUP - 1, :] / weight_sum
    loss[...] = loss_sum / weight_sum


def local(clean, noise, modulation, strata, up_weight, down_weight):
    _, rows_per, features = clean.shape
    sizes = [lax.axis_size(a) for a in ("zb", "zi", "yb", "yi")]
    outer_z, inner_z, outer_y, inner_y = sizes
    size_x = lax.axis_size("x")
    units = up_weight.shape[1]
    share = rows_per // size_x
    shape = jax.ShapeDtypeStruct
    params = pltpu.CompilerParams(vmem_limit_bytes=VMEM)
    call = functools.partial(pl.pallas_call, compiler_params=params)
    other_up = swap_cores(up_weight)
    other_down = swap_cores(down_weight)
    member = lax.axis_index("zi") * inner_y + lax.axis_index("yi")
    place = jnp.stack([lax.axis_index("c"), lax.axis_index("x"), member]).astype(jnp.int32)
    steps = 2
    tile = rows_per // steps
    latent = pl.BlockSpec((1, tile, features), lambda i, place, strata: (place[0], i, 0))
    modulated, info = call(
        modulate_kernel,
        out_shape=(shape((rows_per, features), bf16), shape((2, GROUP, LANES), f32)),
        grid_spec=pltpu.PrefetchScalarGridSpec(
            num_scalar_prefetch=2,
            grid=(steps,),
            in_specs=[
                latent,
                latent,
                pl.BlockSpec(modulation.shape, lambda i, place, strata: (0, 0)),
            ],
            out_specs=[
                pl.BlockSpec((tile, features), lambda i, place, strata: (i, 0)),
                pl.BlockSpec((2, GROUP, LANES), lambda i, place, strata: (0, 0, 0)),
            ],
        ),
        name="modulate",
    )(place, strata, clean, noise, modulation)
    members = inner_z * inner_y
    blocks = [modulated] + [
        lax.ppermute(modulated, ("zi", "yi"), [(i, i ^ k) for i in range(members)])
        for k in range(1, members)
    ]

    ups, downs = (up_weight, other_up), (down_weight, other_down)
    preacts = [jnp.dot(modulated, w, preferred_element_type=f32) for w in ups]
    partial_value = sum(
        jnp.dot(gelu_tanh(p).astype(bf16), w, preferred_element_type=f32)
        for p, w in zip(preacts, downs)
    )
    parts = exchanged(partial_value.astype(bf16).reshape(size_x, share, features), "x")

    share_of = pl.BlockSpec((1, share, features), lambda i, place: (place[0], place[1], 0))
    loss_call = call(
        loss_kernel,
        out_shape=shape((size_x, share, features + LANES), bf16),
        grid_spec=pltpu.PrefetchScalarGridSpec(
            num_scalar_prefetch=1,
            grid=(1,),
            in_specs=[
                pl.BlockSpec(parts.shape, lambda i, place: (0, 0, 0)),
                share_of,
                share_of,
                pl.BlockSpec(modulation.shape, lambda i, place: (0, 0)),
                pl.BlockSpec(info.shape, lambda i, place: (0, 0, 0)),
            ],
            out_specs=pl.BlockSpec(
                (size_x, share, features + LANES), lambda i, place: (0, 0, 0)
            ),
        ),
        name="loss",
    )
    message = loss_call(place, parts, clean, noise, modulation, info)
    message = exchanged(message, "x")

    half = outer_z * outer_y * GROUP
    backward = call(
        functools.partial(backward_kernel, sizes),
        out_shape=shape((members, 2 * half, rows_per), bf16),
        scratch_shapes=[pltpu.VMEM((2 * units + GROUP, rows_per), f32)],
        name="backward",
    )
    pre_slope = backward(message, *downs, *(p.T for p in preacts), info)
    pre_slope = exchanged(pre_slope, ("zi", "yi"))

    whole = pl.BlockSpec(memory_space=pltpu.VMEM)
    scalar = pl.BlockSpec(memory_space=pltpu.SMEM)
    product = functools.partial(call, out_shape=shape((half, features), bf16))
    away = product(away_kernel, in_specs=[scalar] + [whole] * 5, name="away")(
        place, pre_slope, *blocks
    )
    home = product(home_kernel, in_specs=[scalar] + [whole] * 6, name="home")(
        place, pre_slope, swap_cores(away), *blocks
    )
    parts = exchanged(home.reshape(outer_z * outer_y, GROUP, features), ("zb", "yb"))
    gradient, loss = call(
        finish_kernel,
        out_shape=(shape((GROUP - 1, features), f32), shape((1, 1), f32)),
        name="finish",
    )(parts)
    return (gradient, loss[0, 0])


def solution(mesh):
    finer = Mesh(mesh.devices.reshape(6, 2, 4, 2, 4, 2), (*DP, *MP))
    return jax.shard_map(
        local,
        mesh=finer,
        in_specs=(
            P(DP, None, None),
            P(DP, None, None),
            P(DP, None),
            P(DP),
            P(None, MP),
            P(MP, None),
        ),
        out_specs=(P(MP_DP, None), P()),
        check_vma=False,
    )
```

time: 154 us -> 172 us (1.12)
  the two profiles are of different devices: /device:TPU:2 before, /device:TPU:8 now
where the time goes in v2:
time: 172 us; the launch traced here: 171 us
  blocking collectives  84 us (49%)
  starting transfers between devices  27.5 us (16%)
  waiting for transfers between devices  25.5 us (15%)
  Pallas kernels  21.9 us (13%)
  matrix products  7.55 us (4%)
  local copies, waits for them, and re-layouts  3.02 us (2%)
    all_to_all x3, blocking collectives, exchanged(): return lax.all_to_all(array, axis, 0, 0, tiled=True)  84 us
    ppermute x3, waiting for transfers between devices, local(): lax.ppermute(modulated, ('zi', 'yi'), [(i, i ^ k) for i in range(members)])  22.8 us
    all_to_all x1, starting transfers between devices, exchanged(): return lax.all_to_all(array, axis, 0, 0, tiled=True)  12 us
    ppermute x3, starting transfers between devices, local(): lax.ppermute(modulated, ('zi', 'yi'), [(i, i ^ k) for i in range(members)])  9.2 us
    ppermute x3, starting transfers between devices, swap_cores(): return lax.ppermute(array, 'c', [(0, 1), (1, 0)])  6.24 us
    pallas_call x1, Pallas kernels, local(): pre_slope = backward(message, *downs, *(p.T for p in preacts), info)  6.12 us
    dot_general x2, matrix products, local(): preacts = [jnp.dot(modulated, w, preferred_element_type=f32) for w in ups]  6.05 us
    pallas_call x1, Pallas kernels, local(): product(home_kernel, in_specs=[scalar] + [whole] * 6, name='home')  3.68 us
  transfers between devices with their start and end apart: 7, of which 4 were waited for; matrix products, arithmetic and copies ran while one was open for 4% of the time, Pallas kernels for 2%

profile of v2, /device:TPU:8, one launch (start us, length us, event | category | flops | bytes accessed | tf_op | source)
XLA Modules:
  0.0 170.9 jit_solution(17641547630051795489)
XLA Ops:
  0.6 1.9 %collective-permute-start = (bf16[2432,672]{0,1:T(8,128)(2,1)}, bf16[2432,672]{0,1:T(8,128)(2,1)}, u32[]{:S(2)}, u32[]{:S(2)}) collective-permute-start(bf16[2432,672]{0,1:T(8,128)(2,1)} %param.10), channel_id=1, source_target_pairs={{0,1},{1,0},{2,3},{3,2},{4,5},{5,4},{6,7},{7,6},{8,9},{9,8},{10,11... | collective-permute-start | bytes 9805832 | tf_op jit(solution)/shard_map/ppermute | solution.py:27
  2.6 2.4 %collective-permute-start.1 = (bf16[672,2432]{1,0:T(8,128)(2,1)}, bf16[672,2432]{1,0:T(8,128)(2,1)S(1)}, u32[]{:S(2)}, u32[]{:S(2)}) collective-permute-start(bf16[672,2432]{1,0:T(8,128)(2,1)} %down_0.1), channel_id=1, source_target_pairs={{0,1},{1,0},{2,3},{3,2},{4,5},{5,4},{6,7},{7,6},{8,9},{9,8},{10,11... | collective-permute-start | bytes 9805832 | tf_op jit(solution)/shard_map/ppermute | solution.py:27
  5.0 0.7 pad_add_fusion.place
  5.6 3.6 %modulate.1 = (bf16[128,2432]{1,0:T(8,128)(2,1)}, f32[2,8,128]{2,1,0:T(8,128)}) custom-call(s32[3]{0:T(128)} %pad_add_fusion.place, s32[2]{0:T(128)} %strata.1, bf16[2,128,2432]{2,1,0:T(8,128)(2,1)} %clean.3, bf16[2,128,2432]{2,1,0:T(8,128)(2,1)} %noise.3, f32[2,7296]{1,0:T(2,128)} %modulation.3), custom_call_target="tpu_custom_call" | custom-call | tf_op jit(solution)/shard_map/modulate/pallas_call | solution.py:228
  9.2 3.1 %fusion.36 = f32[128,672]{0,1:T(8,128)S(1)} fusion(bf16[128,2432]{1,0:T(8,128)(2,1)} %get-tuple-element.6.refs_0_, bf16[2432,672]{0,1:T(8,128)(2,1)} %param.10), kind=kOutput, calls=%fused_computation.38 | convolution fusion | flops 418381824 | bytes 4235264 | tf_op jit(solution)/shard_map/dot_general | solution.py:253
  12.4 0.7 fusion.18
  13.1 0.0 collective-permute-done
  13.1 0.4 copy-done.2
  13.6 2.9 %fusion.37 = f32[128,672]{0,1:T(8,128)S(1)} fusion(bf16[128,2432]{1,0:T(8,128)(2,1)S(1)} %copy-done.2, bf16[2432,672]{0,1:T(8,128)(2,1)} %collective-permute-done), kind=kOutput, calls=%fused_computation.39 | convolution fusion | flops 418381824 | bytes 4235264 | tf_op jit(solution)/shard_map/dot_general | solution.py:253
  16.5 0.0 collective-permute-done.1.down_1
  16.6 0.8 fusion
  17.3 14.9 %all_to_all.20.parts = bf16[4,32,2432]{2,1,0:T(8,128)(2,1)} all-to-all(bf16[4,32,2432]{2,1,0:T(8,128)(2,1)S(1)} %bitcast.17), channel_id=1, replica_groups=mesh['zb'=6,'zi'=2,'yb'=4,'yi'=2,'x'=4,'c'=2] {'x'}, dimensions={0} | all-to-all | bytes 1245184 | tf_op jit(solution)/shard_map/all_to_all | solution.py:31
  32.2 3.2 %loss.1 = bf16[4,32,2560]{2,1,0:T(8,128)(2,1)} custom-call(s32[3]{0:T(128)} %pad_add_fusion.place, bf16[4,32,2432]{2,1,0:T(8,128)(2,1)} %all_to_all.20.parts, bf16[2,128,2432]{2,1,0:T(8,128)(2,1)} %clean.3, bf16[2,128,2432]{2,1,0:T(8,128)(2,1)} %noise.3, f32[2,7296]{1,0:T(2,128)} %modulation.3, f32[2,8,128]{2,1,0:T(8,128)} %get-tuple-element.7.info), custom_call_target="tpu_custom_call" | custom-call | tf_op jit(solution)/shard_map/loss/pallas_call | solution.py:280
  35.4 14.4 %all_to_all.21.message = bf16[4,32,2560]{2,1,0:T(8,128)(2,1)} all-to-all(bf16[4,32,2560]{2,1,0:T(8,128)(2,1)} %loss.1), channel_id=1, replica_groups=mesh['zb'=6,'zi'=2,'yb'=4,'yi'=2,'x'=4,'c'=2] {'x'}, dimensions={0} | all-to-all | bytes 1310720 | tf_op jit(solution)/shard_map/all_to_all | solution.py:31
  49.8 6.1 %backward.1 = bf16[4,384,128]{2,1,0:T(8,128)(2,1)} custom-call(bf16[4,32,2560]{2,1,0:T(8,128)(2,1)} %all_to_all.21.message, bf16[672,2432]{1,0:T(8,128)(2,1)} %down_0.1, bf16[672,2432]{1,0:T(8,128)(2,1)} %copy-done.1, f32[672,128]{1,0:T(8,128)} %bitcast.15, f32[672,128]{1,0:T(8,128)} %bitcast.16, f32[2,8,128]{2,1,0:T(8,128)} %get-tuple-element.7.info), custom_call_target="tpu_custom_call" | custom-call | tf_op jit(solution)/shard_map/backward/pallas_call | solution.py:290
  55.9 12.0 %all-to-all-start.2 = ((bf16[4,384,128]{2,1,0:T(8,128)(2,1)}), bf16[4,384,128]{2,1,0:T(8,128)(2,1)S(1)}, u32[]{:S(2)}, u32[]{:S(2)}) async-start(bf16[4,384,128]{2,1,0:T(8,128)(2,1)} %backward.1), calls=%async_computation.2 | async-start | bytes 786432 | tf_op jit(solution)/shard_map/all_to_all | solution.py:31
  68.0 2.0 %collective-permute-start.2 = (bf16[128,2432]{1,0:T(8,128)(2,1)S(1)}, bf16[128,2432]{1,0:T(8,128)(2,1)S(1)}, u32[]{:S(2)}, u32[]{:S(2)}) collective-permute-start(bf16[128,2432]{1,0:T(8,128)(2,1)S(1)} %copy-done.3), channel_id=1, source_target_pairs={{0,8},{8,0},{64,72},{72,64},{1,9},{9,1},{65,73},{73,65},{2,10},{10... | collective-permute-start | bytes 1867784 | tf_op jit(solution)/shard_map/ppermute | solution.py:248
  69.9 3.9 %collective-permute-start.3 = (bf16[128,2432]{1,0:T(8,128)(2,1)S(1)}, bf16[128,2432]{1,0:T(8,128)(2,1)S(1)}, u32[]{:S(2)}, u32[]{:S(2)}) collective-permute-start(bf16[128,2432]{1,0:T(8,128)(2,1)S(1)} %copy-done.3), channel_id=1, source_target_pairs={{0,64},{8,72},{64,0},{72,8},{1,65},{9,73},{65,1},{73,9},{2,66},{10... | collective-permute-start | bytes 1867784 | tf_op jit(solution)/shard_map/ppermute | solution.py:248
  73.8 3.4 %collective-permute-start.4 = (bf16[128,2432]{1,0:T(8,128)(2,1)S(1)}, bf16[128,2432]{1,0:T(8,128)(2,1)S(1)}, u32[]{:S(2)}, u32[]{:S(2)}) collective-permute-start(bf16[128,2432]{1,0:T(8,128)(2,1)S(1)} %copy-done.3), channel_id=1, source_target_pairs={{0,72},{8,64},{64,8},{72,0},{1,73},{9,65},{65,9},{73,1},{2,74},{10... | collective-permute-start | bytes 1867784 | tf_op jit(solution)/shard_map/ppermute | solution.py:248
  77.2 10.0 %collective-permute-done.2.refs_1_ = bf16[128,2432]{1,0:T(8,128)(2,1)S(1)} collective-permute-done((bf16[128,2432]{1,0:T(8,128)(2,1)S(1)}, bf16[128,2432]{1,0:T(8,128)(2,1)S(1)}, u32[]{:S(2)}, u32[]{:S(2)}) %collective-permute-start.2) | collective-permute-done | bytes 622624 | tf_op jit(solution)/shard_map/ppermute | solution.py:248
  87.1 1.6 collective-permute-done.3.refs_2_
  88.7 11.3 %collective-permute-done.4.refs_3_ = bf16[128,2432]{1,0:T(8,128)(2,1)S(1)} collective-permute-done((bf16[128,2432]{1,0:T(8,128)(2,1)S(1)}, bf16[128,2432]{1,0:T(8,128)(2,1)S(1)}, u32[]{:S(2)}, u32[]{:S(2)}) %collective-permute-start.4) | collective-permute-done | bytes 622624 | tf_op jit(solution)/shard_map/ppermute | solution.py:248
  100.0 0.0 all-to-all-done.2.pre_slope
  100.0 0.8 copy-done.9
  100.8 0.7 copy-done.4
  101.6 3.4 %away.1 = bf16[192,2432]{1,0:T(8,128)(2,1)} custom-call(s32[3]{0:T(128)} %pad_add_fusion.place, bf16[4,384,128]{2,1,0:T(8,128)(2,1)} %copy-done.4, bf16[128,2432]{1,0:T(8,128)(2,1)} %get-tuple-element.6.refs_0_, bf16[128,2432]{1,0:T(8,128)(2,1)} %copy-done.7, bf16[128,2432]{1,0:T(8,128)(2,1)} %copy-done.8, bf16[128,2432]{1,0:T(8,128)(2,1)} %copy-done.9), custom_call_target="tpu_custom_call" | custom-call | tf_op jit(solution)/shard_map/away/pallas_call | solution.py:296
  105.0 1.9 %collective-permute-start.5 = (bf16[192,2432]{1,0:T(8,128)(2,1)}, bf16[192,2432]{1,0:T(8,128)(2,1)S(1)}, u32[]{:S(2)}, u32[]{:S(2)}) collective-permute-start(bf16[192,2432]{1,0:T(8,128)(2,1)} %away.1), channel_id=1, source_target_pairs={{0,1},{1,0},{2,3},{3,2},{4,5},{5,4},{6,7},{7,6},{8,9},{9,8},{10,11... | collective-permute-start | bytes 2801672 | tf_op jit(solution)/shard_map/ppermute | solution.py:27
  106.9 2.7 %collective-permute-done.5.got = bf16[192,2432]{1,0:T(8,128)(2,1)S(1)} collective-permute-done((bf16[192,2432]{1,0:T(8,128)(2,1)}, bf16[192,2432]{1,0:T(8,128)(2,1)S(1)}, u32[]{:S(2)}, u32[]{:S(2)}) %collective-permute-start.5) | collective-permute-done | bytes 933920 | tf_op jit(solution)/shard_map/ppermute | solution.py:27
  109.6 1.0 copy-done.10
  110.6 3.7 %home.1 = bf16[192,2432]{1,0:T(8,128)(2,1)} custom-call(s32[3]{0:T(128)} %pad_add_fusion.place, bf16[4,384,128]{2,1,0:T(8,128)(2,1)} %copy-done.4, bf16[192,2432]{1,0:T(8,128)(2,1)} %copy-done.10, bf16[128,2432]{1,0:T(8,128)(2,1)} %get-tuple-element.6.refs_0_, bf16[128,2432]{1,0:T(8,128)(2,1)} %copy-done.7, bf16[128,2432]{1,0:T(8,128)(2,1)} %copy-done.8, ...), custom_call_target="tpu_custom_call" | custom-call | tf_op jit(solution)/shard_map/home/pallas_call | solution.py:299
  114.2 54.7 %all_to_all.22.parts = bf16[24,8,2432]{2,1,0:T(8,128)(2,1)} all-to-all(bf16[24,8,2432]{2,1,0:T(8,128)(2,1)} %bitcast.14), channel_id=1, replica_groups=mesh['zb'=6,'zi'=2,'yb'=4,'yi'=2,'x'=4,'c'=2] {'zb','yb'}, dimensions={0} | all-to-all | bytes 1867776 | tf_op jit(solution)/shard_map/all_to_all | solution.py:31
  169.0 2.0 %finish.1 = (f32[7,2432]{1,0:T(8,128)}, f32[1,1]{1,0:T(1,128)}) custom-call(bf16[24,8,2432]{2,1,0:T(8,128)(2,1)} %all_to_all.22.parts), custom_call_target="tpu_custom_call" | custom-call | tf_op jit(solution)/shard_map/finish/pallas_call | solution.py:303
  (18 shorter events, 0.0 us)
Async XLA Ops:
  0.6 12.5 %collective-permute-start = (bf16[2432,672]{0,1:T(8,128)(2,1)}, bf16[2432,672]{0,1:T(8,128)(2,1)}, u32[]{:S(2)}, u32[]{:S(2)}) collective-permute-start(bf16[2432,672]{0,1:T(8,128)(2,1)} %param.10), channel_id=1, source_target_pairs={{0,1},{1,0},{2,3},{3,2},{4,5},{5,4},{6,7},{7,6},{8,9},{9,8},{10,11... | collective-permute-start | bytes 9805832 | tf_op jit(solution)/shard_map/ppermute | solution.py:27
  2.6 14.0 %collective-permute-start.1 = (bf16[672,2432]{1,0:T(8,128)(2,1)}, bf16[672,2432]{1,0:T(8,128)(2,1)S(1)}, u32[]{:S(2)}, u32[]{:S(2)}) collective-permute-start(bf16[672,2432]{1,0:T(8,128)(2,1)} %down_0.1), channel_id=1, source_target_pairs={{0,1},{1,0},{2,3},{3,2},{4,5},{5,4},{6,7},{7,6},{8,9},{9,8},{10,11... | collective-permute-start | bytes 9805832 | tf_op jit(solution)/shard_map/ppermute | solution.py:27
  5.6 6.7 %copy-start = (bf16[672,2432]{1,0:T(8,128)(2,1)S(1)}, bf16[672,2432]{1,0:T(8,128)(2,1)}, u32[]{:S(2)}) copy-start(bf16[672,2432]{1,0:T(8,128)(2,1)} %down_0.1) | copy-start | bytes 9805828
  12.4 4.1 %copy-start.5 = (f32[128,672]{0,1:T(8,128)}, f32[128,672]{0,1:T(8,128)S(1)}, u32[]{:S(2)}) copy-start(f32[128,672]{0,1:T(8,128)S(1)} %fusion.36) | copy-start | bytes 1032196
  12.4 1.2 copy-start.2
  16.5 15.7 %copy-start.6 = (f32[128,672]{0,1:T(8,128)}, f32[128,672]{0,1:T(8,128)S(1)}, u32[]{:S(2)}) copy-start(f32[128,672]{0,1:T(8,128)S(1)} %fusion.37) | copy-start | bytes 1032196
  16.5 15.7 %copy-start.1 = (bf16[672,2432]{1,0:T(8,128)(2,1)}, bf16[672,2432]{1,0:T(8,128)(2,1)S(1)}, u32[]{:S(2)}) copy-start(bf16[672,2432]{1,0:T(8,128)(2,1)S(1)} %collective-permute-done.1.down_1) | copy-start | bytes 9805828
  49.8 18.2 %copy-start.3 = (bf16[128,2432]{1,0:T(8,128)(2,1)S(1)}, bf16[128,2432]{1,0:T(8,128)(2,1)}, u32[]{:S(2)}) copy-start(bf16[128,2432]{1,0:T(8,128)(2,1)} %get-tuple-element.6.refs_0_) | copy-start | bytes 1867780
  55.9 44.1 %all-to-all-start.2 = ((bf16[4,384,128]{2,1,0:T(8,128)(2,1)}), bf16[4,384,128]{2,1,0:T(8,128)(2,1)S(1)}, u32[]{:S(2)}, u32[]{:S(2)}) async-start(bf16[4,384,128]{2,1,0:T(8,128)(2,1)} %backward.1), calls=%async_computation.2 | async-start | bytes 786432 | tf_op jit(solution)/shard_map/all_to_all | solution.py:31
  68.0 19.2 %collective-permute-start.2 = (bf16[128,2432]{1,0:T(8,128)(2,1)S(1)}, bf16[128,2432]{1,0:T(8,128)(2,1)S(1)}, u32[]{:S(2)}, u32[]{:S(2)}) collective-permute-start(bf16[128,2432]{1,0:T(8,128)(2,1)S(1)} %copy-done.3), channel_id=1, source_target_pairs={{0,8},{8,0},{64,72},{72,64},{1,9},{9,1},{65,73},{73,65},{2,10},{10... | collective-permute-start | bytes 1867784 | tf_op jit(solution)/shard_map/ppermute | solution.py:248
  69.9 18.8 %collective-permute-start.3 = (bf16[128,2432]{1,0:T(8,128)(2,1)S(1)}, bf16[128,2432]{1,0:T(8,128)(2,1)S(1)}, u32[]{:S(2)}, u32[]{:S(2)}) collective-permute-start(bf16[128,2432]{1,0:T(8,128)(2,1)S(1)} %copy-done.3), channel_id=1, source_target_pairs={{0,64},{8,72},{64,0},{72,8},{1,65},{9,73},{65,1},{73,9},{2,66},{10... | collective-permute-start | bytes 1867784 | tf_op jit(solution)/shard_map/ppermute | solution.py:248
  73.8 26.2 %collective-permute-start.4 = (bf16[128,2432]{1,0:T(8,128)(2,1)S(1)}, bf16[128,2432]{1,0:T(8,128)(2,1)S(1)}, u32[]{:S(2)}, u32[]{:S(2)}) collective-permute-start(bf16[128,2432]{1,0:T(8,128)(2,1)S(1)} %copy-done.3), channel_id=1, source_target_pairs={{0,72},{8,64},{64,8},{72,0},{1,73},{9,65},{65,9},{73,1},{2,74},{10... | collective-permute-start | bytes 1867784 | tf_op jit(solution)/shard_map/ppermute | solution.py:248
  87.1 12.9 %copy-start.7 = (bf16[128,2432]{1,0:T(8,128)(2,1)}, bf16[128,2432]{1,0:T(8,128)(2,1)S(1)}, u32[]{:S(2)}) copy-start(bf16[128,2432]{1,0:T(8,128)(2,1)S(1)} %collective-permute-done.2.refs_1_) | copy-start | bytes 1867780
  88.7 11.3 %copy-start.8 = (bf16[128,2432]{1,0:T(8,128)(2,1)}, bf16[128,2432]{1,0:T(8,128)(2,1)S(1)}, u32[]{:S(2)}) copy-start(bf16[128,2432]{1,0:T(8,128)(2,1)S(1)} %collective-permute-done.3.refs_2_) | copy-start | bytes 1867780
  100.0 0.8 copy-start.9
  100.8 0.7 copy-start.4
  105.0 4.6 %collective-permute-start.5 = (bf16[192,2432]{1,0:T(8,128)(2,1)}, bf16[192,2432]{1,0:T(8,128)(2,1)S(1)}, u32[]{:S(2)}, u32[]{:S(2)}) collective-permute-start(bf16[192,2432]{1,0:T(8,128)(2,1)} %away.1), channel_id=1, source_target_pairs={{0,1},{1,0},{2,3},{3,2},{4,5},{5,4},{6,7},{7,6},{8,9},{9,8},{10,11... | collective-permute-start | bytes 2801672 | tf_op jit(solution)/shard_map/ppermute | solution.py:27
  109.6 1.0 copy-start.10

commit v3 on v2

--- a/solution.py
+++ b/solution.py
@@ -16,11 +16,19 @@
 MP_DP = (*MP, *DP)
 LANES = 128
 GROUP = 8
-VMEM = 56 * 2**20
+VMEM = 16 * 2**20
 
 loss_scale = 1048576.0
 f32 = jnp.float32
 bf16 = jnp.bfloat16
+
+
+def near(*arrays):
+    return [pltpu.with_memory_space_constraint(a, pltpu.VMEM) for a in arrays]
+
+
+def far(*arrays):
+    return [pltpu.with_memory_space_constraint(a, pltpu.HBM) for a in arrays]
 
 
 def swap_cores(array):
@@ -87,7 +95,7 @@
     return (noisy_field, drift_field - anchor)
 
 
-def modulate_kernel(place, strata, clean, noise, modulation, modulated, info):
+def modulate_kernel(place, strata, clean, noise, modulation, modulated, info, noisy, target):
     features = clean.shape[-1]
     core = place[0]
     stratum = jnp.full((GROUP, LANES), strata[core].astype(f32), f32)
@@ -106,19 +114,51 @@
     shift = modulation[pl.ds(core, 1), :features]
     scale = modulation[pl.ds(core, 1), features : 2 * features]
     modulated[...] = (normed * (1.0 + scale) + shift).astype(bf16)
-
-
-def loss_kernel(place, parts, clean, noise, modulation, info, message):
+    share = noisy.shape[0]
+    shares = clean.shape[1] // share
+
+    @pl.when(place[1] // shares == pl.program_id(0))
+    def _():
+        rows = pl.ds(pl.multiple_of(place[1] % shares * share, share), share)
+        noisy[...], target[...] = blend(clean[0, rows, :], noise[0, rows, :], fraction[:1, :1])
+
+
+def forward_kernel(rows, up_0, up_1, down_0, down_1, out, pre_0, pre_1, *scratch):
+    held, arrived = scratch[:3], scratch[3]
+    copies = [
+        pltpu.make_async_copy(source, place, arrived.at[k])
+        for k, (source, place) in enumerate(zip((up_0, up_1, down_0), held))
+    ]
+    for copy in copies:
+        copy.start()
+    hidden = []
+    for k, pre in enumerate((pre_0, pre_1)):
+        copies[k].wait()
+        preact = lax.dot_general(
+            held[k][...], rows[...], (((1,), (1,)), ((), ())), preferred_element_type=f32
+        )
+        pre[...] = preact
+        hidden.append(gelu_tanh(preact).astype(bf16))
+    parts = lax.dot_general(
+        hidden[1], down_1[...], (((0,), (0,)), ((), ())), preferred_element_type=f32
+    )
+    copies[2].wait()
+    parts = parts + lax.dot_general(
+        hidden[0], held[2][...], (((0,), (0,)), ((), ())), preferred_element_type=f32
+    )
+    out[...] = parts.astype(bf16)
+
+
+def loss_kernel(place, parts, noisy, target, modulation, info, message):
     copies, share, features = parts.shape
-    fraction, weight = info[0][:1, :1], info[1][:1, :1]
+    weight = info[1][:1, :1]
     gate = modulation[pl.ds(place[0], 1), 2 * features :]
     output = parts[0].astype(f32)
     for j in range(1, copies):
         output = output + parts[j].astype(f32)
-    noisy_share, target_share = blend(clean[0], noise[0], fraction)
-    errors = noisy_share + gate * output - target_share
+    errors = noisy[...] + gate * output - target[...]
     squares = jnp.sum(jnp.sum(errors * errors, axis=0, keepdims=True), axis=1, keepdims=True)
-    rows = clean.shape[1] * copies
+    rows = share * copies
     loss_local = weight * squares / (rows * features)
     coefficient = (loss_scale * 2.0 / (rows * features)) * weight
     slopes = (coefficient * gate * errors).astype(bf16)
@@ -151,7 +191,7 @@
             halves = []
             for k in (at, at + 1):
                 r, owner = divmod(k, outer_z * outer_y)
-                zb, yb = divmod(owner, outer_y)
+                yb, zb = divmod(owner, outer_z)
                 owner = ((zb * inner_z + zi) * outer_y + yb) * inner_y + yi
                 start = r * units + owner * group
                 halves.append(flat[start : start + GROUP, :])
@@ -190,21 +230,50 @@
 
 
 def home_kernel(place, pre_slope, got, *refs):
-    *blocks, out = refs
-    half = out.shape[0]
+    *blocks, out, flat = refs
+    pieces, rows, _ = out.shape
+    half, features = got.shape
+    tiles = features // LANES
+    kept = GROUP - 1
     product = gathered_product(place, pre_slope, blocks, 0, half)
     got_row = got[:GROUP, :LANES].astype(f32)[GROUP - 1 :, :]
     sums = [a + decoded(got_row, k) for k, a in enumerate(gathered_sums(pre_slope))]
-    store_marked(out, product + got[...].astype(f32), sums)
-
-
-def finish_kernel(parts, gradient, loss):
+    last = jnp.broadcast_to(coded_row(sums), (rows - kept * tiles, LANES))
+    joined = product + got[...].astype(f32)
+    for p in range(pieces):
+        for t in range(tiles):
+            block = joined[p * GROUP : (p + 1) * GROUP, t * LANES : (t + 1) * LANES]
+            start = p * rows + t * kept
+            flat[start : start + GROUP, :] = block
+        flat[p * rows + kept * tiles : (p + 1) * rows, :] = last
+        out[p] = flat[p * rows : (p + 1) * rows, :].astype(bf16)
+
+
+def middle_kernel(kept, parts, out):
+    pieces, rows, _ = out.shape
     total = parts[0].astype(f32)
     for j in range(1, parts.shape[0]):
         total = total + parts[j].astype(f32)
-    row = total[GROUP - 1 :, :LANES]
+    row = total[kept : kept + 1, :]
+    scalars = coded_row([decoded(row, k) for k in range(2)])
+    place = lax.broadcasted_iota(jnp.int32, (rows, LANES), 0)
+    for p in range(pieces):
+        block = total[p * rows : (p + 1) * rows, :]
+        out[p] = jnp.where(place >= kept, scalars, block).astype(bf16)
+
+
+def finish_kernel(parts, gradient, loss, flat):
+    kept, features = gradient.shape
+    tiles = features // LANES
+    total = parts[0].astype(f32)
+    for j in range(1, parts.shape[0]):
+        total = total + parts[j].astype(f32)
+    flat[: total.shape[0], :] = total
+    row = flat[kept * tiles : kept * tiles + 1, :]
     loss_sum, weight_sum = decoded(row, 0), decoded(row, 1)
-    gradient[...] = total[: GROUP - 1, :] / weight_sum
+    for t in range(tiles):
+        block = flat[t * kept : t * kept + GROUP, :]
+        gradient[:, t * LANES : (t + 1) * LANES] = (block / weight_sum)[:kept, :]
     loss[...] = loss_sum / weight_sum
 
 
@@ -225,86 +294,100 @@
     steps = 2
     tile = rows_per // steps
     latent = pl.BlockSpec((1, tile, features), lambda i, place, strata: (place[0], i, 0))
-    modulated, info = call(
+    fixed = lambda array: pl.BlockSpec(array.shape, lambda i, *_: (0,) * len(array.shape))
+    kept_rows = shape((share, features), f32)
+    levels = shape((2, GROUP, LANES), f32)
+    modulated, info, noisy, target = call(
         modulate_kernel,
-        out_shape=(shape((rows_per, features), bf16), shape((2, GROUP, LANES), f32)),
+        out_shape=(shape((rows_per, features), bf16), levels, kept_rows, kept_rows),
         grid_spec=pltpu.PrefetchScalarGridSpec(
             num_scalar_prefetch=2,
             grid=(steps,),
-            in_specs=[
-                latent,
-                latent,
-                pl.BlockSpec(modulation.shape, lambda i, place, strata: (0, 0)),
-            ],
+            in_specs=[latent, latent, fixed(modulation)],
             out_specs=[
-                pl.BlockSpec((tile, features), lambda i, place, strata: (i, 0)),
-                pl.BlockSpec((2, GROUP, LANES), lambda i, place, strata: (0, 0, 0)),
+                pl.BlockSpec((tile, features), lambda i, *_: (i, 0)),
+                *(fixed(a) for a in (levels, kept_rows, kept_rows)),
             ],
         ),
         name="modulate",
-    )(place, strata, clean, noise, modulation)
+    )(place, *far(strata, clean, noise, modulation))
     members = inner_z * inner_y
     blocks = [modulated] + [
         lax.ppermute(modulated, ("zi", "yi"), [(i, i ^ k) for i in range(members)])
         for k in range(1, members)
     ]
 
-    ups, downs = (up_weight, other_up), (down_weight, other_down)
-    preacts = [jnp.dot(modulated, w, preferred_element_type=f32) for w in ups]
-    partial_value = sum(
-        jnp.dot(gelu_tanh(p).astype(bf16), w, preferred_element_type=f32)
-        for p, w in zip(preacts, downs)
-    )
-    parts = exchanged(partial_value.astype(bf16).reshape(size_x, share, features), "x")
-
-    share_of = pl.BlockSpec((1, share, features), lambda i, place: (place[0], place[1], 0))
+    whole = pl.BlockSpec(memory_space=pltpu.VMEM)
+    away_from = pl.BlockSpec(memory_space=pl.ANY)
+    ups, downs = (up_weight.T, other_up.T), (down_weight, other_down)
+    preact = pltpu.VMEM((units, rows_per), f32)
+    forward = call(
+        forward_kernel,
+        out_shape=(pltpu.VMEM((rows_per, features), bf16), preact, preact),
+        in_specs=[whole, away_from, away_from, away_from, whole],
+        scratch_shapes=[
+            *(pltpu.VMEM((units, features), bf16) for _ in range(3)),
+            pltpu.SemaphoreType.DMA((3,)),
+        ],
+        name="forward",
+    )
+    partial_value, *preacts = forward(
+        modulated, *far(*ups, down_weight), *near(other_down)
+    )
+    parts = exchanged(partial_value.reshape(size_x, share, features), "x")
+
+    scalar = pl.BlockSpec(memory_space=pltpu.SMEM)
     loss_call = call(
         loss_kernel,
-        out_shape=shape((size_x, share, features + LANES), bf16),
-        grid_spec=pltpu.PrefetchScalarGridSpec(
-            num_scalar_prefetch=1,
-            grid=(1,),
-            in_specs=[
-                pl.BlockSpec(parts.shape, lambda i, place: (0, 0, 0)),
-                share_of,
-                share_of,
-                pl.BlockSpec(modulation.shape, lambda i, place: (0, 0)),
-                pl.BlockSpec(info.shape, lambda i, place: (0, 0, 0)),
-            ],
-            out_specs=pl.BlockSpec(
-                (size_x, share, features + LANES), lambda i, place: (0, 0, 0)
-            ),
-        ),
+        out_shape=pltpu.VMEM((size_x, share, features + LANES), bf16),
+        in_specs=[scalar] + [whole] * 5,
         name="loss",
     )
-    message = loss_call(place, parts, clean, noise, modulation, info)
+    message = loss_call(place, *near(parts, noisy, target, modulation, info))
     message = exchanged(message, "x")
 
     half = outer_z * outer_y * GROUP
     backward = call(
         functools.partial(backward_kernel, sizes),
         out_shape=shape((members, 2 * half, rows_per), bf16),
+        in_specs=[whole] * 6,
         scratch_shapes=[pltpu.VMEM((2 * units + GROUP, rows_per), f32)],
         name="backward",
     )
-    pre_slope = backward(message, *downs, *(p.T for p in preacts), info)
+    pre_slope = backward(*near(message, *downs, *preacts, info))
     pre_slope = exchanged(pre_slope, ("zi", "yi"))
 
-    whole = pl.BlockSpec(memory_space=pltpu.VMEM)
-    scalar = pl.BlockSpec(memory_space=pltpu.SMEM)
-    product = functools.partial(call, out_shape=shape((half, features), bf16))
-    away = product(away_kernel, in_specs=[scalar] + [whole] * 5, name="away")(
-        place, pre_slope, *blocks
-    )
-    home = product(home_kernel, in_specs=[scalar] + [whole] * 6, name="home")(
-        place, pre_slope, swap_cores(away), *blocks
-    )
-    parts = exchanged(home.reshape(outer_z * outer_y, GROUP, features), ("zb", "yb"))
+    pre_slope, *blocks = near(pre_slope, *blocks)
+    away = call(
+        away_kernel,
+        out_shape=pltpu.VMEM((half, features), bf16),
+        in_specs=[scalar] + [whole] * (1 + members),
+        name="away",
+    )(place, pre_slope, *blocks)
+    pieces = outer_z * outer_y
+    flat_rows = -(-((GROUP - 1) * features // LANES + 1) // GROUP) * GROUP
+    home = call(
+        home_kernel,
+        out_shape=pltpu.VMEM((pieces, flat_rows, LANES), bf16),
+        in_specs=[scalar] + [whole] * (2 + members),
+        scratch_shapes=[pltpu.VMEM((pieces * flat_rows, LANES), f32)],
+        name="home",
+    )(place, pre_slope, *near(swap_cores(away)), *blocks)
+    parts = exchanged(home.reshape(outer_y, outer_z * flat_rows, LANES), "yb")
+    middle = call(
+        functools.partial(middle_kernel, (GROUP - 1) * features // LANES),
+        out_shape=pltpu.VMEM((outer_z, flat_rows, LANES), bf16),
+        in_specs=[whole],
+        name="middle",
+    )(*near(parts))
+    parts = exchanged(middle, "zb")
     gradient, loss = call(
         finish_kernel,
         out_shape=(shape((GROUP - 1, features), f32), shape((1, 1), f32)),
+        in_specs=[whole],
+        scratch_shapes=[pltpu.VMEM((flat_rows, LANES), f32)],
         name="finish",
-    )(parts)
+    )(*near(parts))
     return (gradient, loss[0, 0])
 
 

time: 172 us -> 156 us (0.907)
  matrix products: 7.55 us -> 0 us
  blocking collectives: 84 us -> 76.7 us
  waiting for transfers between devices: 25.5 us -> 31.5 us
  Pallas kernels: 21.9 us -> 16.1 us
    dot_general x4 -> x0, matrix products: 7.55 us -> none  [the longest x2 6.05 us: local(): preacts = [jnp.dot(modulated, w, preferred_element_type=f32) for w in ups]]
    all_to_all x3 -> x4, blocking collectives: 84 us -> 76.7 us  [exchanged(): return lax.all_to_all(array, axis, 0, 0, tiled=True)]
    ppermute x3, waiting for transfers between devices: 2.68 us -> 8.09 us  [swap_cores(): return lax.ppermute(array, 'c', [(0, 1), (1, 0)])]
    pallas_call x5 -> x7, Pallas kernels: 20 us -> 15.4 us  [the longest x1 6.91 us: local(): forward(modulated, *far(*ups, down_weight), *near(other_down))]
  transfers between devices with their start and end apart: 7 -> 7, of which waited for: 4 -> 6; matrix products, arithmetic and copies ran while one was open for 4% -> 0% of each run, Pallas kernels for 2% -> 2%
where the time goes in v3:
time: 156 us; the launch traced here: 155 us
  blocking collectives  76.7 us (49%)
  waiting for transfers between devices  31.5 us (20%)
  starting transfers between devices  27.5 us (18%)
  Pallas kernels  16.1 us (10%)
  local copies, waits for them, and re-layouts  2.67 us (2%)
    all_to_all x4, blocking collectives, exchanged(): return lax.all_to_all(array, axis, 0, 0, tiled=True)  76.7 us
    ppermute x3, waiting for transfers between devices, local(): lax.ppermute(modulated, ('zi', 'yi'), [(i, i ^ k) for i in range(members)])  23.4 us
    all_to_all x1, starting transfers between devices, exchanged(): return lax.all_to_all(array, axis, 0, 0, tiled=True)  12.1 us
    ppermute x3, starting transfers between devices, local(): lax.ppermute(modulated, ('zi', 'yi'), [(i, i ^ k) for i in range(members)])  9.2 us
    ppermute x3, waiting for transfers between devices, swap_cores(): return lax.ppermute(array, 'c', [(0, 1), (1, 0)])  8.09 us
    pallas_call x1, Pallas kernels, local(): forward(modulated, *far(*ups, down_weight), *near(other_down))  6.91 us
    ppermute x3, starting transfers between devices, swap_cores(): return lax.ppermute(array, 'c', [(0, 1), (1, 0)])  6.25 us
  transfers between devices with their start and end apart: 7, of which 6 were waited for; matrix products, arithmetic and copies ran while one was open for 0% of the time, Pallas kernels for 2%

profile of v3, /device:TPU:8, one launch (start us, length us, event | category | flops | bytes accessed | tf_op | source)
XLA Modules:
  0.0 155.4 jit_solution(5202091281700472942)
XLA Ops:
  0.6 1.9 %collective-permute-start.1 = (bf16[672,2432]{1,0:T(8,128)(2,1)}, bf16[672,2432]{1,0:T(8,128)(2,1)S(1)}, u32[]{:S(2)}, u32[]{:S(2)}) collective-permute-start(bf16[672,2432]{1,0:T(8,128)(2,1)} %down_0.3), channel_id=1, source_target_pairs={{0,1},{1,0},{2,3},{3,2},{4,5},{5,4},{6,7},{7,6},{8,9},{9,8},{10,11... | collective-permute-start | bytes 9805832 | tf_op jit(solution)/shard_map/ppermute | solution.py:35
  2.6 2.4 %collective-permute-start = (bf16[2432,672]{0,1:T(8,128)(2,1)}, bf16[2432,672]{0,1:T(8,128)(2,1)}, u32[]{:S(2)}, u32[]{:S(2)}) collective-permute-start(bf16[2432,672]{0,1:T(8,128)(2,1)} %param.10), channel_id=1, source_target_pairs={{0,1},{1,0},{2,3},{3,2},{4,5},{5,4},{6,7},{7,6},{8,9},{9,8},{10,11... | collective-permute-start | bytes 9805832 | tf_op jit(solution)/shard_map/ppermute | solution.py:35
  5.0 0.1 pad_add_fusion.place
  5.1 2.7 %modulate.1 = (bf16[128,2432]{1,0:T(8,128)(2,1)S(1)}, f32[2,8,128]{2,1,0:T(8,128)S(1)}, f32[32,2432]{1,0:T(8,128)S(1)}, f32[32,2432]{1,0:T(8,128)S(1)}) custom-call(s32[3]{0:T(128)S(1)} %pad_add_fusion.place, s32[2]{0:T(128)} %strata.1, bf16[2,128,2432]{2,1,0:T(8,128)(2,1)} %clean.1, bf16[2,128,2432]{2,1,0:T(8,128)(2,1)} %noise.1, f32[2,7296]{1,0:T(2,128)} %modulation.3), custom_call_target="tpu_custom_call" | custom-call | tf_op jit(solution)/shard_map/modulate/pallas_call | solution.py:300
  7.7 0.8 collective-permute-done.1.down_1
  8.6 4.8 %collective-permute-done = bf16[2432,672]{0,1:T(8,128)(2,1)} collective-permute-done((bf16[2432,672]{0,1:T(8,128)(2,1)}, bf16[2432,672]{0,1:T(8,128)(2,1)}, u32[]{:S(2)}, u32[]{:S(2)}) %collective-permute-start) | collective-permute-done | bytes 3268640 | tf_op jit(solution)/shard_map/ppermute | solution.py:35
  13.4 6.9 %forward.1 = (bf16[128,2432]{1,0:T(8,128)(2,1)S(1)}, f32[672,128]{1,0:T(8,128)S(1)}, f32[672,128]{1,0:T(8,128)S(1)}) custom-call(bf16[128,2432]{1,0:T(8,128)(2,1)S(1)} %get-tuple-element.11.rows.refs_0_, bf16[672,2432]{1,0:T(8,128)(2,1)} %bitcast.10, bf16[672,2432]{1,0:T(8,128)(2,1)} %bitcast.4.up_1, bf16[672,2432]{1,0:T(8,128)(2,1)} %down_0.3, ...), custom_call_target="tpu_custom_call" | custom-call | tf_op jit(solution)/shard_map/forward/pallas_call | solution.py:334
  20.3 0.0 copy-start.1
  20.3 0.8 copy-done.1
  21.1 15.2 %all_to_all.25.parts = bf16[4,32,2432]{2,1,0:T(8,128)(2,1)S(1)} all-to-all(bf16[4,32,2432]{2,1,0:T(8,128)(2,1)S(1)} %bitcast.9), channel_id=1, replica_groups=mesh['zb'=6,'zi'=2,'yb'=4,'yi'=2,'x'=4,'c'=2] {'x'}, dimensions={0} | all-to-all | bytes 1245184 | tf_op jit(solution)/shard_map/all_to_all | solution.py:39
  36.3 0.0 copy-done.5
  36.3 0.9 loss.1
  37.2 12.5 %all_to_all.26.message = bf16[4,32,2560]{2,1,0:T(8,128)(2,1)S(1)} all-to-all(bf16[4,32,2560]{2,1,0:T(8,128)(2,1)S(1)} %loss.1), channel_id=1, replica_groups=mesh['zb'=6,'zi'=2,'yb'=4,'yi'=2,'x'=4,'c'=2] {'x'}, dimensions={0} | all-to-all | bytes 1310720 | tf_op jit(solution)/shard_map/all_to_all | solution.py:39
  49.7 2.1 %backward.1 = bf16[4,384,128]{2,1,0:T(8,128)(2,1)S(1)} custom-call(bf16[4,32,2560]{2,1,0:T(8,128)(2,1)S(1)} %all_to_all.26.message, bf16[672,2432]{1,0:T(8,128)(2,1)S(1)} %copy-done, bf16[672,2432]{1,0:T(8,128)(2,1)S(1)} %collective-permute-done.1.down_1, f32[672,128]{1,0:T(8,128)S(1)} %get-tuple-element.16.pre_0, f32[672,128]{1,0:T(8,128)S(1)} %get-tuple-element.17.pre_1, ...), custom_call_target="tpu_custom_call" | custom-call | tf_op jit(solution)/shard_map/backward/pallas_call | solution.py:357
  51.9 0.8 copy-done.4
  52.6 12.1 %all-to-all-start.2 = ((bf16[4,384,128]{2,1,0:T(8,128)(2,1)}), bf16[4,384,128]{2,1,0:T(8,128)(2,1)S(1)}, u32[]{:S(2)}, u32[]{:S(2)}) async-start(bf16[4,384,128]{2,1,0:T(8,128)(2,1)} %copy-done.4), calls=%async_computation.2 | async-start | bytes 786432 | tf_op jit(solution)/shard_map/all_to_all | solution.py:39
  64.7 1.9 %collective-permute-start.2 = (bf16[128,2432]{1,0:T(8,128)(2,1)}, bf16[128,2432]{1,0:T(8,128)(2,1)S(1)}, u32[]{:S(2)}, u32[]{:S(2)}) collective-permute-start(bf16[128,2432]{1,0:T(8,128)(2,1)} %copy-done.1), channel_id=1, source_target_pairs={{0,8},{8,0},{64,72},{72,64},{1,9},{9,1},{65,73},{73,65},{2,10},{10... | collective-permute-start | bytes 1867784 | tf_op jit(solution)/shard_map/ppermute | solution.py:316
  66.7 3.9 %collective-permute-start.3 = (bf16[128,2432]{1,0:T(8,128)(2,1)}, bf16[128,2432]{1,0:T(8,128)(2,1)S(1)}, u32[]{:S(2)}, u32[]{:S(2)}) collective-permute-start(bf16[128,2432]{1,0:T(8,128)(2,1)} %copy-done.1), channel_id=1, source_target_pairs={{0,64},{8,72},{64,0},{72,8},{1,65},{9,73},{65,1},{73,9},{2,66},{10... | collective-permute-start | bytes 1867784 | tf_op jit(solution)/shard_map/ppermute | solution.py:316
  70.5 3.4 %collective-permute-start.4 = (bf16[128,2432]{1,0:T(8,128)(2,1)}, bf16[128,2432]{1,0:T(8,128)(2,1)S(1)}, u32[]{:S(2)}, u32[]{:S(2)}) collective-permute-start(bf16[128,2432]{1,0:T(8,128)(2,1)} %copy-done.1), channel_id=1, source_target_pairs={{0,72},{8,64},{64,8},{72,0},{1,73},{9,65},{65,9},{73,1},{2,74},{10... | collective-permute-start | bytes 1867784 | tf_op jit(solution)/shard_map/ppermute | solution.py:316
  73.9 9.1 %collective-permute-done.2.refs_1_ = bf16[128,2432]{1,0:T(8,128)(2,1)S(1)} collective-permute-done((bf16[128,2432]{1,0:T(8,128)(2,1)}, bf16[128,2432]{1,0:T(8,128)(2,1)S(1)}, u32[]{:S(2)}, u32[]{:S(2)}) %collective-permute-start.2) | collective-permute-done | bytes 622624 | tf_op jit(solution)/shard_map/ppermute | solution.py:316
  83.0 2.7 %collective-permute-done.3.refs_2_ = bf16[128,2432]{1,0:T(8,128)(2,1)S(1)} collective-permute-done((bf16[128,2432]{1,0:T(8,128)(2,1)}, bf16[128,2432]{1,0:T(8,128)(2,1)S(1)}, u32[]{:S(2)}, u32[]{:S(2)}) %collective-permute-start.3) | collective-permute-done | bytes 622624 | tf_op jit(solution)/shard_map/ppermute | solution.py:316
  85.7 11.7 %collective-permute-done.4.refs_3_ = bf16[128,2432]{1,0:T(8,128)(2,1)S(1)} collective-permute-done((bf16[128,2432]{1,0:T(8,128)(2,1)}, bf16[128,2432]{1,0:T(8,128)(2,1)S(1)}, u32[]{:S(2)}, u32[]{:S(2)}) %collective-permute-start.4) | collective-permute-done | bytes 622624 | tf_op jit(solution)/shard_map/ppermute | solution.py:316
  97.3 0.0 all-to-all-done.2.pre_slope
  97.3 1.1 copy-done.2
  98.4 1.2 away.1
  99.6 1.9 %collective-permute-start.5 = (bf16[192,2432]{1,0:T(8,128)(2,1)S(1)}, bf16[192,2432]{1,0:T(8,128)(2,1)S(1)}, u32[]{:S(2)}, u32[]{:S(2)}) collective-permute-start(bf16[192,2432]{1,0:T(8,128)(2,1)S(1)} %away.1), channel_id=1, source_target_pairs={{0,1},{1,0},{2,3},{3,2},{4,5},{5,4},{6,7},{7,6},{8,9},{9,8},{10,11... | collective-permute-start | bytes 2801672 | tf_op jit(solution)/shard_map/ppermute | solution.py:35
  101.6 2.5 %collective-permute-done.5.got = bf16[192,2432]{1,0:T(8,128)(2,1)S(1)} collective-permute-done((bf16[192,2432]{1,0:T(8,128)(2,1)S(1)}, bf16[192,2432]{1,0:T(8,128)(2,1)S(1)}, u32[]{:S(2)}, u32[]{:S(2)}) %collective-permute-start.5) | collective-permute-done | bytes 933920 | tf_op jit(solution)/shard_map/ppermute | solution.py:35
  104.0 1.4 home.1
  105.4 26.4 %all_to_all.27.parts = bf16[4,816,128]{2,1,0:T(8,128)(2,1)S(1)} all-to-all(bf16[4,816,128]{2,1,0:T(8,128)(2,1)S(1)} %bitcast.8), channel_id=1, replica_groups=mesh['zb'=6,'zi'=2,'yb'=4,'yi'=2,'x'=4,'c'=2] {'yb'}, dimensions={0} | all-to-all | bytes 1671168 | tf_op jit(solution)/shard_map/all_to_all | solution.py:39
  131.8 0.2 middle.1
  132.0 22.7 %all_to_all.28.parts = bf16[6,136,128]{2,1,0:T(8,128)(2,1)S(1)} all-to-all(bf16[6,136,128]{2,1,0:T(8,128)(2,1)S(1)} %middle.1), channel_id=1, replica_groups=mesh['zb'=6,'zi'=2,'yb'=4,'yi'=2,'x'=4,'c'=2] {'zb'}, dimensions={0} | all-to-all | bytes 417792 | tf_op jit(solution)/shard_map/all_to_all | solution.py:39
  154.6 0.7 finish.1
  (7 shorter events, 0.0 us)
Async XLA Ops:
  0.6 7.9 %collective-permute-start.1 = (bf16[672,2432]{1,0:T(8,128)(2,1)}, bf16[672,2432]{1,0:T(8,128)(2,1)S(1)}, u32[]{:S(2)}, u32[]{:S(2)}) collective-permute-start(bf16[672,2432]{1,0:T(8,128)(2,1)} %down_0.3), channel_id=1, source_target_pairs={{0,1},{1,0},{2,3},{3,2},{4,5},{5,4},{6,7},{7,6},{8,9},{9,8},{10,11... | collective-permute-start | bytes 9805832 | tf_op jit(solution)/shard_map/ppermute | solution.py:35
  2.6 10.8 %collective-permute-start = (bf16[2432,672]{0,1:T(8,128)(2,1)}, bf16[2432,672]{0,1:T(8,128)(2,1)}, u32[]{:S(2)}, u32[]{:S(2)}) collective-permute-start(bf16[2432,672]{0,1:T(8,128)(2,1)} %param.10), channel_id=1, source_target_pairs={{0,1},{1,0},{2,3},{3,2},{4,5},{5,4},{6,7},{7,6},{8,9},{9,8},{10,11... | collective-permute-start | bytes 9805832 | tf_op jit(solution)/shard_map/ppermute | solution.py:35
  13.4 22.9 %copy-start.5 = (f32[2,7296]{1,0:T(2,128)S(1)}, f32[2,7296]{1,0:T(2,128)}, u32[]{:S(2)}) copy-start(f32[2,7296]{1,0:T(2,128)} %modulation.3) | copy-start | bytes 175108
  20.3 0.8 copy-start.1
  21.1 28.6 %copy-start = (bf16[672,2432]{1,0:T(8,128)(2,1)S(1)}, bf16[672,2432]{1,0:T(8,128)(2,1)}, u32[]{:S(2)}) copy-start(bf16[672,2432]{1,0:T(8,128)(2,1)} %down_0.3) | copy-start | bytes 9805828
  51.9 0.8 copy-start.4
  52.6 51.4 %copy-start.3 = (bf16[128,2432]{1,0:T(8,128)(2,1)S(1)}, bf16[128,2432]{1,0:T(8,128)(2,1)}, u32[]{:S(2)}) copy-start(bf16[128,2432]{1,0:T(8,128)(2,1)} %copy-done.1) | copy-start | bytes 1867780
  52.6 44.7 %all-to-all-start.2 = ((bf16[4,384,128]{2,1,0:T(8,128)(2,1)}), bf16[4,384,128]{2,1,0:T(8,128)(2,1)S(1)}, u32[]{:S(2)}, u32[]{:S(2)}) async-start(bf16[4,384,128]{2,1,0:T(8,128)(2,1)} %copy-done.4), calls=%async_computation.2 | async-start | bytes 786432 | tf_op jit(solution)/shard_map/all_to_all | solution.py:39
  64.7 18.3 %collective-permute-start.2 = (bf16[128,2432]{1,0:T(8,128)(2,1)}, bf16[128,2432]{1,0:T(8,128)(2,1)S(1)}, u32[]{:S(2)}, u32[]{:S(2)}) collective-permute-start(bf16[128,2432]{1,0:T(8,128)(2,1)} %copy-done.1), channel_id=1, source_target_pairs={{0,8},{8,0},{64,72},{72,64},{1,9},{9,1},{65,73},{73,65},{2,10},{10... | collective-permute-start | bytes 1867784 | tf_op jit(solution)/shard_map/ppermute | solution.py:316
  66.7 19.0 %collective-permute-start.3 = (bf16[128,2432]{1,0:T(8,128)(2,1)}, bf16[128,2432]{1,0:T(8,128)(2,1)S(1)}, u32[]{:S(2)}, u32[]{:S(2)}) collective-permute-start(bf16[128,2432]{1,0:T(8,128)(2,1)} %copy-done.1), channel_id=1, source_target_pairs={{0,64},{8,72},{64,0},{72,8},{1,65},{9,73},{65,1},{73,9},{2,66},{10... | collective-permute-start | bytes 1867784 | tf_op jit(solution)/shard_map/ppermute | solution.py:316
  70.5 26.8 %collective-permute-start.4 = (bf16[128,2432]{1,0:T(8,128)(2,1)}, bf16[128,2432]{1,0:T(8,128)(2,1)S(1)}, u32[]{:S(2)}, u32[]{:S(2)}) collective-permute-start(bf16[128,2432]{1,0:T(8,128)(2,1)} %copy-done.1), channel_id=1, source_target_pairs={{0,72},{8,64},{64,8},{72,0},{1,73},{9,65},{65,9},{73,1},{2,74},{10... | collective-permute-start | bytes 1867784 | tf_op jit(solution)/shard_map/ppermute | solution.py:316
  97.3 1.1 copy-start.2
  99.6 4.4 %collective-permute-start.5 = (bf16[192,2432]{1,0:T(8,128)(2,1)S(1)}, bf16[192,2432]{1,0:T(8,128)(2,1)S(1)}, u32[]{:S(2)}, u32[]{:S(2)}) collective-permute-start(bf16[192,2432]{1,0:T(8,128)(2,1)S(1)} %away.1), channel_id=1, source_target_pairs={{0,1},{1,0},{2,3},{3,2},{4,5},{5,4},{6,7},{7,6},{8,9},{9,8},{10,11... | collective-permute-start | bytes 2801672 | tf_op jit(solution)/shard_map/ppermute | solution.py:35

commit v4 on v3

--- a/solution.py
+++ b/solution.py
@@ -168,14 +168,18 @@
         message[j, :, features:] = side
 
 
-def backward_kernel(sizes, message, down_0, down_1, pre_0, pre_1, info, out, flat):
+def backward_kernel(sizes, message, down_0, down_1, pre_0, pre_1, info, out, flat, held, arrived):
     outer_z, inner_z, outer_y, inner_y = sizes
     copies, share, width = message.shape
     features = width - LANES
     units = pre_0.shape[0]
     group = units // math.prod(sizes)
+    fetch = pltpu.make_async_copy(down_1, held, arrived)
+    fetch.start()
     slopes = message[:, :, :features].reshape(copies * share, features)
-    for r, (down, pre) in enumerate(((down_0, pre_0), (down_1, pre_1))):
+    for r, (down, pre) in enumerate(((down_0, pre_0), (held, pre_1))):
+        if r == 1:
+            fetch.wait()
         hidden_slope = lax.dot_general(
             down[...], slopes, (((1,), (1,)), ((), ())), preferred_element_type=f32
         )
@@ -295,11 +299,11 @@
     tile = rows_per // steps
     latent = pl.BlockSpec((1, tile, features), lambda i, place, strata: (place[0], i, 0))
     fixed = lambda array: pl.BlockSpec(array.shape, lambda i, *_: (0,) * len(array.shape))
-    kept_rows = shape((share, features), f32)
-    levels = shape((2, GROUP, LANES), f32)
+    kept_rows = pltpu.HBM((share, features), f32)
+    levels = pltpu.HBM((2, GROUP, LANES), f32)
     modulated, info, noisy, target = call(
         modulate_kernel,
-        out_shape=(shape((rows_per, features), bf16), levels, kept_rows, kept_rows),
+        out_shape=(pltpu.HBM((rows_per, features), bf16), levels, kept_rows, kept_rows),
         grid_spec=pltpu.PrefetchScalarGridSpec(
             num_scalar_prefetch=2,
             grid=(steps,),
@@ -319,11 +323,12 @@
 
     whole = pl.BlockSpec(memory_space=pltpu.VMEM)
     away_from = pl.BlockSpec(memory_space=pl.ANY)
-    ups, downs = (up_weight.T, other_up.T), (down_weight, other_down)
-    preact = pltpu.VMEM((units, rows_per), f32)
-    forward = call(
+    ups = (up_weight.T, other_up.T)
+    preact = pltpu.HBM((units, rows_per), f32)
+    forward = pl.pallas_call(
         forward_kernel,
-        out_shape=(pltpu.VMEM((rows_per, features), bf16), preact, preact),
+        compiler_params=pltpu.CompilerParams(vmem_limit_bytes=24 * 2**20),
+        out_shape=(pltpu.HBM((rows_per, features), bf16), preact, preact),
         in_specs=[whole, away_from, away_from, away_from, whole],
         scratch_shapes=[
             *(pltpu.VMEM((units, features), bf16) for _ in range(3)),
@@ -332,7 +337,7 @@
         name="forward",
     )
     partial_value, *preacts = forward(
-        modulated, *far(*ups, down_weight), *near(other_down)
+        *far(modulated, *ups, down_weight), *near(other_down)
     )
     parts = exchanged(partial_value.reshape(size_x, share, features), "x")
 
@@ -343,21 +348,27 @@
         in_specs=[scalar] + [whole] * 5,
         name="loss",
     )
-    message = loss_call(place, *near(parts, noisy, target, modulation, info))
+    message = loss_call(place, *far(parts, noisy, target), *near(modulation, info))
     message = exchanged(message, "x")
 
     half = outer_z * outer_y * GROUP
     backward = call(
         functools.partial(backward_kernel, sizes),
-        out_shape=shape((members, 2 * half, rows_per), bf16),
-        in_specs=[whole] * 6,
-        scratch_shapes=[pltpu.VMEM((2 * units + GROUP, rows_per), f32)],
+        out_shape=pltpu.HBM((members, 2 * half, rows_per), bf16),
+        in_specs=[whole, whole, away_from, whole, whole, whole],
+        scratch_shapes=[
+            pltpu.VMEM((2 * units + GROUP, rows_per), f32),
+            pltpu.VMEM((units, features), bf16),
+            pltpu.SemaphoreType.DMA(()),
+        ],
         name="backward",
     )
-    pre_slope = backward(*near(message, *downs, *preacts, info))
+    pre_slope = backward(
+        *near(message, down_weight), *far(other_down), *near(*preacts, info)
+    )
     pre_slope = exchanged(pre_slope, ("zi", "yi"))
 
-    pre_slope, *blocks = near(pre_slope, *blocks)
+    pre_slope, *blocks = *near(pre_slope), *far(*blocks)
     away = call(
         away_kernel,
         out_shape=pltpu.VMEM((half, features), bf16),

time: 156 us -> 162 us (1.038)
  Pallas kernels: 16.1 us -> 24.5 us
  local copies, waits for them, and re-layouts: 2.67 us -> 0.86 us
    pallas_call x4, Pallas kernels: 12.6 us -> 18.8 us  [the longest x1 8.82 us: local(): forward(*far(modulated, *ups, down_weight), *near(other_down))]
    unnamed x12 -> x20, local copies, waits for them, and re-layouts: 2.67 us -> 0.86 us
  transfers between devices with their start and end apart: 7 -> 7, of which waited for: 6 -> 5; matrix products, arithmetic and copies ran while one was open for 0% -> 0% of each run, Pallas kernels for 2% -> 2%
where the time goes in v4:
time: 162 us; the launch traced here: 161 us
  blocking collectives  75.8 us (47%)
  waiting for transfers between devices  30.3 us (19%)
  starting transfers between devices  28.8 us (18%)
  Pallas kernels  24.5 us (15%)
    all_to_all x4, blocking collectives, exchanged(): return lax.all_to_all(array, axis, 0, 0, tiled=True)  75.8 us
    ppermute x3, waiting for transfers between devices, local(): lax.ppermute(modulated, ('zi', 'yi'), [(i, i ^ k) for i in range(members)])  23.2 us
    all_to_all x1, starting transfers between devices, exchanged(): return lax.all_to_all(array, axis, 0, 0, tiled=True)  13.4 us
    ppermute x3, starting transfers between devices, local(): lax.ppermute(modulated, ('zi', 'yi'), [(i, i ^ k) for i in range(members)])  9.2 us
    pallas_call x1, Pallas kernels, local(): forward(*far(modulated, *ups, down_weight), *near(other_down))  8.82 us
    ppermute x3, waiting for transfers between devices, swap_cores(): return lax.ppermute(array, 'c', [(0, 1), (1, 0)])  7.14 us
    ppermute x3, starting transfers between devices, swap_cores(): return lax.ppermute(array, 'c', [(0, 1), (1, 0)])  6.25 us
    pallas_call x1, Pallas kernels, local(): backward(*near(message, down_weight), *far(other_down), *near(*preacts, i...  4.69 us
  transfers between devices with their start and end apart: 7, of which 5 were waited for; matrix products, arithmetic and copies ran while one was open for 0% of the time, Pallas kernels for 2%

profile of v4, /device:TPU:8, one launch (start us, length us, event | category | flops | bytes accessed | tf_op | source)
XLA Modules:
  0.0 161.2 jit_solution(14962954504501032761)
XLA Ops:
  0.6 1.9 %collective-permute-start.1 = (bf16[672,2432]{1,0:T(8,128)(2,1)}, bf16[672,2432]{1,0:T(8,128)(2,1)S(1)}, u32[]{:S(2)}, u32[]{:S(2)}) collective-permute-start(bf16[672,2432]{1,0:T(8,128)(2,1)} %down_0.3), channel_id=1, source_target_pairs={{0,1},{1,0},{2,3},{3,2},{4,5},{5,4},{6,7},{7,6},{8,9},{9,8},{10,11... | collective-permute-start | bytes 9805832 | tf_op jit(solution)/shard_map/ppermute | solution.py:35
  2.6 2.4 %collective-permute-start = (bf16[2432,672]{0,1:T(8,128)(2,1)}, bf16[2432,672]{0,1:T(8,128)(2,1)}, u32[]{:S(2)}, u32[]{:S(2)}) collective-permute-start(bf16[2432,672]{0,1:T(8,128)(2,1)} %param.10), channel_id=1, source_target_pairs={{0,1},{1,0},{2,3},{3,2},{4,5},{5,4},{6,7},{7,6},{8,9},{9,8},{10,11... | collective-permute-start | bytes 9805832 | tf_op jit(solution)/shard_map/ppermute | solution.py:35
  5.0 0.1 pad_add_fusion.place
  5.1 3.6 %modulate.1 = (bf16[128,2432]{1,0:T(8,128)(2,1)}, f32[2,8,128]{2,1,0:T(8,128)}, f32[32,2432]{1,0:T(8,128)}, f32[32,2432]{1,0:T(8,128)}) custom-call(s32[3]{0:T(128)S(1)} %pad_add_fusion.place, s32[2]{0:T(128)} %strata.1, bf16[2,128,2432]{2,1,0:T(8,128)(2,1)} %clean.1, bf16[2,128,2432]{2,1,0:T(8,128)(2,1)} %noise.1, f32[2,7296]{1,0:T(2,128)} %modulation.3), custom_call_target="tpu_custom_call" | custom-call | tf_op jit(solution)/shard_map/modulate/pallas_call | solution.py:304
  8.7 0.0 collective-permute-done.1.down_1
  8.7 4.7 %collective-permute-done = bf16[2432,672]{0,1:T(8,128)(2,1)} collective-permute-done((bf16[2432,672]{0,1:T(8,128)(2,1)}, bf16[2432,672]{0,1:T(8,128)(2,1)}, u32[]{:S(2)}, u32[]{:S(2)}) %collective-permute-start) | collective-permute-done | bytes 3268640 | tf_op jit(solution)/shard_map/ppermute | solution.py:35
  13.4 8.8 %forward.1 = (bf16[128,2432]{1,0:T(8,128)(2,1)}, f32[672,128]{1,0:T(8,128)}, f32[672,128]{1,0:T(8,128)}) custom-call(bf16[128,2432]{1,0:T(8,128)(2,1)} %get-tuple-element.11.rows.refs_0_, bf16[672,2432]{1,0:T(8,128)(2,1)} %bitcast.9, bf16[672,2432]{1,0:T(8,128)(2,1)} %bitcast.4.up_1, bf16[672,2432]{1,0:T(8,128)(2,1)} %down_0.3, ...), custom_call_target="tpu_custom_call" | custom-call | tf_op jit(solution)/shard_map/forward/pallas_call | solution.py:339
  22.2 0.0 copy-start
  22.3 15.6 %all_to_all.25.parts = bf16[4,32,2432]{2,1,0:T(8,128)(2,1)} all-to-all(bf16[4,32,2432]{2,1,0:T(8,128)(2,1)} %bitcast.10), channel_id=1, replica_groups=mesh['zb'=6,'zi'=2,'yb'=4,'yi'=2,'x'=4,'c'=2] {'x'}, dimensions={0} | all-to-all | bytes 1245184 | tf_op jit(solution)/shard_map/all_to_all | solution.py:39
  37.8 0.0 copy-done.4
  37.8 1.6 %loss.1 = bf16[4,32,2560]{2,1,0:T(8,128)(2,1)S(1)} custom-call(s32[3]{0:T(128)S(1)} %pad_add_fusion.place, bf16[4,32,2432]{2,1,0:T(8,128)(2,1)} %all_to_all.25.parts, f32[32,2432]{1,0:T(8,128)} %get-tuple-element.13.noisy, f32[32,2432]{1,0:T(8,128)} %get-tuple-element.14.target, f32[2,7296]{1,0:T(2,128)S(1)} %copy-done.4, f32[2,8,128]{2,1,0:T(8,128)S(1)} %copy-done.5), custom_call_target="tpu_custom_call" | custom-call | tf_op jit(solution)/shard_map/loss/pallas_call | solution.py:351
  39.5 12.5 %all_to_all.26.message = bf16[4,32,2560]{2,1,0:T(8,128)(2,1)S(1)} all-to-all(bf16[4,32,2560]{2,1,0:T(8,128)(2,1)S(1)} %loss.1), channel_id=1, replica_groups=mesh['zb'=6,'zi'=2,'yb'=4,'yi'=2,'x'=4,'c'=2] {'x'}, dimensions={0} | all-to-all | bytes 1310720 | tf_op jit(solution)/shard_map/all_to_all | solution.py:39
  52.0 0.0 copy-done.3
  52.0 4.7 %backward.1 = bf16[4,384,128]{2,1,0:T(8,128)(2,1)} custom-call(bf16[4,32,2560]{2,1,0:T(8,128)(2,1)S(1)} %all_to_all.26.message, bf16[672,2432]{1,0:T(8,128)(2,1)S(1)} %copy-done, bf16[672,2432]{1,0:T(8,128)(2,1)} %copy-done.1, f32[672,128]{1,0:T(8,128)S(1)} %copy-done.2, f32[672,128]{1,0:T(8,128)S(1)} %copy-done.3, f32[2,8,128]{2,1,0:T(8,128)S(1)} %copy-done.5), custom_call_target="tpu_custom_call" | custom-call | tf_op jit(solution)/shard_map/backward/pallas_call | solution.py:366
  56.7 13.4 %all-to-all-start.2 = ((bf16[4,384,128]{2,1,0:T(8,128)(2,1)}), bf16[4,384,128]{2,1,0:T(8,128)(2,1)S(1)}, u32[]{:S(2)}, u32[]{:S(2)}) async-start(bf16[4,384,128]{2,1,0:T(8,128)(2,1)} %backward.1), calls=%async_computation.2 | async-start | bytes 786432 | tf_op jit(solution)/shard_map/all_to_all | solution.py:39
  70.1 2.0 %collective-permute-start.2 = (bf16[128,2432]{1,0:T(8,128)(2,1)S(1)}, bf16[128,2432]{1,0:T(8,128)(2,1)S(1)}, u32[]{:S(2)}, u32[]{:S(2)}) collective-permute-start(bf16[128,2432]{1,0:T(8,128)(2,1)S(1)} %copy-done.6), channel_id=1, source_target_pairs={{0,8},{8,0},{64,72},{72,64},{1,9},{9,1},{65,73},{73,65},{2,10},{10... | collective-permute-start | bytes 1867784 | tf_op jit(solution)/shard_map/ppermute | solution.py:320
  72.1 3.9 %collective-permute-start.3 = (bf16[128,2432]{1,0:T(8,128)(2,1)S(1)}, bf16[128,2432]{1,0:T(8,128)(2,1)S(1)}, u32[]{:S(2)}, u32[]{:S(2)}) collective-permute-start(bf16[128,2432]{1,0:T(8,128)(2,1)S(1)} %copy-done.6), channel_id=1, source_target_pairs={{0,64},{8,72},{64,0},{72,8},{1,65},{9,73},{65,1},{73,9},{2,66},{10... | collective-permute-start | bytes 1867784 | tf_op jit(solution)/shard_map/ppermute | solution.py:320
  75.9 3.4 %collective-permute-start.4 = (bf16[128,2432]{1,0:T(8,128)(2,1)S(1)}, bf16[128,2432]{1,0:T(8,128)(2,1)S(1)}, u32[]{:S(2)}, u32[]{:S(2)}) collective-permute-start(bf16[128,2432]{1,0:T(8,128)(2,1)S(1)} %copy-done.6), channel_id=1, source_target_pairs={{0,72},{8,64},{64,8},{72,0},{1,73},{9,65},{65,9},{73,1},{2,74},{10... | collective-permute-start | bytes 1867784 | tf_op jit(solution)/shard_map/ppermute | solution.py:320
  79.3 9.2 %collective-permute-done.2.refs_1_ = bf16[128,2432]{1,0:T(8,128)(2,1)S(1)} collective-permute-done((bf16[128,2432]{1,0:T(8,128)(2,1)S(1)}, bf16[128,2432]{1,0:T(8,128)(2,1)S(1)}, u32[]{:S(2)}, u32[]{:S(2)}) %collective-permute-start.2) | collective-permute-done | bytes 622624 | tf_op jit(solution)/shard_map/ppermute | solution.py:320
  88.5 2.3 %collective-permute-done.3.refs_2_ = bf16[128,2432]{1,0:T(8,128)(2,1)S(1)} collective-permute-done((bf16[128,2432]{1,0:T(8,128)(2,1)S(1)}, bf16[128,2432]{1,0:T(8,128)(2,1)S(1)}, u32[]{:S(2)}, u32[]{:S(2)}) %collective-permute-start.3) | collective-permute-done | bytes 622624 | tf_op jit(solution)/shard_map/ppermute | solution.py:320
  90.9 11.6 %collective-permute-done.4.refs_3_ = bf16[128,2432]{1,0:T(8,128)(2,1)S(1)} collective-permute-done((bf16[128,2432]{1,0:T(8,128)(2,1)S(1)}, bf16[128,2432]{1,0:T(8,128)(2,1)S(1)}, u32[]{:S(2)}, u32[]{:S(2)}) %collective-permute-start.4) | collective-permute-done | bytes 622624 | tf_op jit(solution)/shard_map/ppermute | solution.py:320
  102.5 0.0 all-to-all-done.2.pre_slope
  102.5 0.0 copy-done.8
  102.5 0.8 copy-done.9
  103.3 2.3 %away.1 = bf16[192,2432]{1,0:T(8,128)(2,1)S(1)} custom-call(s32[3]{0:T(128)S(1)} %pad_add_fusion.place, bf16[4,384,128]{2,1,0:T(8,128)(2,1)S(1)} %all-to-all-done.2.pre_slope, bf16[128,2432]{1,0:T(8,128)(2,1)} %get-tuple-element.11.rows.refs_0_, bf16[128,2432]{1,0:T(8,128)(2,1)} %copy-done.7, bf16[128,2432]{1,0:T(8,128)(2,1)} %copy-done.8, ...), custom_call_target="tpu_custom_call" | custom-call | tf_op jit(solution)/shard_map/away/pallas_call | solution.py:372
  105.7 1.9 %collective-permute-start.5 = (bf16[192,2432]{1,0:T(8,128)(2,1)S(1)}, bf16[192,2432]{1,0:T(8,128)(2,1)S(1)}, u32[]{:S(2)}, u32[]{:S(2)}) collective-permute-start(bf16[192,2432]{1,0:T(8,128)(2,1)S(1)} %away.1), channel_id=1, source_target_pairs={{0,1},{1,0},{2,3},{3,2},{4,5},{5,4},{6,7},{7,6},{8,9},{9,8},{10,11... | collective-permute-start | bytes 2801672 | tf_op jit(solution)/shard_map/ppermute | solution.py:35
  107.6 2.5 %collective-permute-done.5.got = bf16[192,2432]{1,0:T(8,128)(2,1)S(1)} collective-permute-done((bf16[192,2432]{1,0:T(8,128)(2,1)S(1)}, bf16[192,2432]{1,0:T(8,128)(2,1)S(1)}, u32[]{:S(2)}, u32[]{:S(2)}) %collective-permute-start.5) | collective-permute-done | bytes 933920 | tf_op jit(solution)/shard_map/ppermute | solution.py:35
  110.1 2.5 %home.1 = bf16[24,136,128]{2,1,0:T(8,128)(2,1)S(1)} custom-call(s32[3]{0:T(128)S(1)} %pad_add_fusion.place, bf16[4,384,128]{2,1,0:T(8,128)(2,1)S(1)} %all-to-all-done.2.pre_slope, bf16[192,2432]{1,0:T(8,128)(2,1)S(1)} %collective-permute-done.5.got, bf16[128,2432]{1,0:T(8,128)(2,1)} %get-tuple-element.11.rows.refs_0_, bf16[128,2432]{1,0:T(8,128)(2,1)} %copy-done.7, ...), custom_call_target="tpu_custom_call" | custom-call | tf_op jit(solution)/shard_map/home/pallas_call | solution.py:380
  112.6 26.7 %all_to_all.27.parts = bf16[4,816,128]{2,1,0:T(8,128)(2,1)S(1)} all-to-all(bf16[4,816,128]{2,1,0:T(8,128)(2,1)S(1)} %bitcast.8), channel_id=1, replica_groups=mesh['zb'=6,'zi'=2,'yb'=4,'yi'=2,'x'=4,'c'=2] {'yb'}, dimensions={0} | all-to-all | bytes 1671168 | tf_op jit(solution)/shard_map/all_to_all | solution.py:39
  139.2 0.2 middle.1
  139.4 21.0 %all_to_all.28.parts = bf16[6,136,128]{2,1,0:T(8,128)(2,1)S(1)} all-to-all(bf16[6,136,128]{2,1,0:T(8,128)(2,1)S(1)} %middle.1), channel_id=1, replica_groups=mesh['zb'=6,'zi'=2,'yb'=4,'yi'=2,'x'=4,'c'=2] {'zb'}, dimensions={0} | all-to-all | bytes 417792 | tf_op jit(solution)/shard_map/all_to_all | solution.py:39
  160.4 0.7 finish.1
  (15 shorter events, 0.0 us)
Async XLA Ops:
  0.6 8.1 %collective-permute-start.1 = (bf16[672,2432]{1,0:T(8,128)(2,1)}, bf16[672,2432]{1,0:T(8,128)(2,1)S(1)}, u32[]{:S(2)}, u32[]{:S(2)}) collective-permute-start(bf16[672,2432]{1,0:T(8,128)(2,1)} %down_0.3), channel_id=1, source_target_pairs={{0,1},{1,0},{2,3},{3,2},{4,5},{5,4},{6,7},{7,6},{8,9},{9,8},{10,11... | collective-permute-start | bytes 9805832 | tf_op jit(solution)/shard_map/ppermute | solution.py:35
  2.6 10.8 %collective-permute-start = (bf16[2432,672]{0,1:T(8,128)(2,1)}, bf16[2432,672]{0,1:T(8,128)(2,1)}, u32[]{:S(2)}, u32[]{:S(2)}) collective-permute-start(bf16[2432,672]{0,1:T(8,128)(2,1)} %param.10), channel_id=1, source_target_pairs={{0,1},{1,0},{2,3},{3,2},{4,5},{5,4},{6,7},{7,6},{8,9},{9,8},{10,11... | collective-permute-start | bytes 9805832 | tf_op jit(solution)/shard_map/ppermute | solution.py:35
  8.7 13.5 %copy-start.1 = (bf16[672,2432]{1,0:T(8,128)(2,1)}, bf16[672,2432]{1,0:T(8,128)(2,1)S(1)}, u32[]{:S(2)}) copy-start(bf16[672,2432]{1,0:T(8,128)(2,1)S(1)} %collective-permute-done.1.down_1) | copy-start | bytes 9805828
  13.4 24.5 %copy-start.4 = (f32[2,7296]{1,0:T(2,128)S(1)}, f32[2,7296]{1,0:T(2,128)}, u32[]{:S(2)}) copy-start(f32[2,7296]{1,0:T(2,128)} %modulation.3) | copy-start | bytes 175108
  13.4 24.5 %copy-start.5 = (f32[2,8,128]{2,1,0:T(8,128)S(1)}, f32[2,8,128]{2,1,0:T(8,128)}, u32[]{:S(2)}) copy-start(f32[2,8,128]{2,1,0:T(8,128)} %get-tuple-element.15.info) | copy-start | bytes 24580
  22.2 29.8 %copy-start = (bf16[672,2432]{1,0:T(8,128)(2,1)S(1)}, bf16[672,2432]{1,0:T(8,128)(2,1)}, u32[]{:S(2)}) copy-start(bf16[672,2432]{1,0:T(8,128)(2,1)} %down_0.3) | copy-start | bytes 9805828
  22.2 29.8 %copy-start.2 = (f32[672,128]{1,0:T(8,128)S(1)}, f32[672,128]{1,0:T(8,128)}, u32[]{:S(2)}) copy-start(f32[672,128]{1,0:T(8,128)} %get-tuple-element.16.pre_0) | copy-start | bytes 1032196
  22.2 29.8 %copy-start.3 = (f32[672,128]{1,0:T(8,128)S(1)}, f32[672,128]{1,0:T(8,128)}, u32[]{:S(2)}) copy-start(f32[672,128]{1,0:T(8,128)} %get-tuple-element.17.pre_1) | copy-start | bytes 1032196
  52.0 18.1 %copy-start.6 = (bf16[128,2432]{1,0:T(8,128)(2,1)S(1)}, bf16[128,2432]{1,0:T(8,128)(2,1)}, u32[]{:S(2)}) copy-start(bf16[128,2432]{1,0:T(8,128)(2,1)} %get-tuple-element.11.rows.refs_0_) | copy-start | bytes 1867780
  56.7 45.8 %all-to-all-start.2 = ((bf16[4,384,128]{2,1,0:T(8,128)(2,1)}), bf16[4,384,128]{2,1,0:T(8,128)(2,1)S(1)}, u32[]{:S(2)}, u32[]{:S(2)}) async-start(bf16[4,384,128]{2,1,0:T(8,128)(2,1)} %backward.1), calls=%async_computation.2 | async-start | bytes 786432 | tf_op jit(solution)/shard_map/all_to_all | solution.py:39
  70.1 18.5 %collective-permute-start.2 = (bf16[128,2432]{1,0:T(8,128)(2,1)S(1)}, bf16[128,2432]{1,0:T(8,128)(2,1)S(1)}, u32[]{:S(2)}, u32[]{:S(2)}) collective-permute-start(bf16[128,2432]{1,0:T(8,128)(2,1)S(1)} %copy-done.6), channel_id=1, source_target_pairs={{0,8},{8,0},{64,72},{72,64},{1,9},{9,1},{65,73},{73,65},{2,10},{10... | collective-permute-start | bytes 1867784 | tf_op jit(solution)/shard_map/ppermute | solution.py:320
  72.1 18.8 %collective-permute-start.3 = (bf16[128,2432]{1,0:T(8,128)(2,1)S(1)}, bf16[128,2432]{1,0:T(8,128)(2,1)S(1)}, u32[]{:S(2)}, u32[]{:S(2)}) collective-permute-start(bf16[128,2432]{1,0:T(8,128)(2,1)S(1)} %copy-done.6), channel_id=1, source_target_pairs={{0,64},{8,72},{64,0},{72,8},{1,65},{9,73},{65,1},{73,9},{2,66},{10... | collective-permute-start | bytes 1867784 | tf_op jit(solution)/shard_map/ppermute | solution.py:320
  75.9 26.6 %collective-permute-start.4 = (bf16[128,2432]{1,0:T(8,128)(2,1)S(1)}, bf16[128,2432]{1,0:T(8,128)(2,1)S(1)}, u32[]{:S(2)}, u32[]{:S(2)}) collective-permute-start(bf16[128,2432]{1,0:T(8,128)(2,1)S(1)} %copy-done.6), channel_id=1, source_target_pairs={{0,72},{8,64},{64,8},{72,0},{1,73},{9,65},{65,9},{73,1},{2,74},{10... | collective-permute-start | bytes 1867784 | tf_op jit(solution)/shard_map/ppermute | solution.py:320
  88.5 14.0 %copy-start.7 = (bf16[128,2432]{1,0:T(8,128)(2,1)}, bf16[128,2432]{1,0:T(8,128)(2,1)S(1)}, u32[]{:S(2)}) copy-start(bf16[128,2432]{1,0:T(8,128)(2,1)S(1)} %collective-permute-done.2.refs_1_) | copy-start | bytes 1867780
  90.9 11.7 %copy-start.8 = (bf16[128,2432]{1,0:T(8,128)(2,1)}, bf16[128,2432]{1,0:T(8,128)(2,1)S(1)}, u32[]{:S(2)}) copy-start(bf16[128,2432]{1,0:T(8,128)(2,1)S(1)} %collective-permute-done.3.refs_2_) | copy-start | bytes 1867780
  102.5 0.8 copy-start.9
  105.7 4.4 %collective-permute-start.5 = (bf16[192,2432]{1,0:T(8,128)(2,1)S(1)}, bf16[192,2432]{1,0:T(8,128)(2,1)S(1)}, u32[]{:S(2)}, u32[]{:S(2)}) collective-permute-start(bf16[192,2432]{1,0:T(8,128)(2,1)S(1)} %away.1), channel_id=1, source_target_pairs={{0,1},{1,0},{2,3},{3,2},{4,5},{5,4},{6,7},{7,6},{8,9},{9,8},{10,11... | collective-permute-start | bytes 2801672 | tf_op jit(solution)/shard_map/ppermute | solution.py:35

commit v5 on v3

--- a/solution.py
+++ b/solution.py
@@ -95,8 +95,15 @@
     return (noisy_field, drift_field - anchor)
 
 
-def modulate_kernel(place, strata, clean, noise, modulation, modulated, info, noisy, target):
+def modulate_kernel(place, strata, clean, noise, modulation, up, *rest):
+    modulated, info, noisy, target, up_near, rows_near, arrived = rest
     features = clean.shape[-1]
+    fetch = pltpu.make_async_copy(up, up_near, arrived)
+
+    @pl.when(pl.program_id(0) == 0)
+    def _():
+        fetch.start()
+
     core = place[0]
     stratum = jnp.full((GROUP, LANES), strata[core].astype(f32), f32)
     level = math.sqrt(2.0) * erf_inverse(2.0 * ((stratum + 0.5) / STRATA) - 1.0)
@@ -113,7 +120,11 @@
     normed = centred * lax.rsqrt(variance + 1e-06)
     shift = modulation[pl.ds(core, 1), :features]
     scale = modulation[pl.ds(core, 1), features : 2 * features]
-    modulated[...] = (normed * (1.0 + scale) + shift).astype(bf16)
+    tile = clean.shape[1]
+    at = pl.ds(pl.multiple_of(pl.program_id(0) * tile, tile), tile)
+    rows_here = (normed * (1.0 + scale) + shift).astype(bf16)
+    modulated[...] = rows_here
+    rows_near[at, :] = rows_here
     share = noisy.shape[0]
     shares = clean.shape[1] // share
 
@@ -122,31 +133,9 @@
         rows = pl.ds(pl.multiple_of(place[1] % shares * share, share), share)
         noisy[...], target[...] = blend(clean[0, rows, :], noise[0, rows, :], fraction[:1, :1])
 
-
-def forward_kernel(rows, up_0, up_1, down_0, down_1, out, pre_0, pre_1, *scratch):
-    held, arrived = scratch[:3], scratch[3]
-    copies = [
-        pltpu.make_async_copy(source, place, arrived.at[k])
-        for k, (source, place) in enumerate(zip((up_0, up_1, down_0), held))
-    ]
-    for copy in copies:
-        copy.start()
-    hidden = []
-    for k, pre in enumerate((pre_0, pre_1)):
-        copies[k].wait()
-        preact = lax.dot_general(
-            held[k][...], rows[...], (((1,), (1,)), ((), ())), preferred_element_type=f32
-        )
-        pre[...] = preact
-        hidden.append(gelu_tanh(preact).astype(bf16))
-    parts = lax.dot_general(
-        hidden[1], down_1[...], (((0,), (0,)), ((), ())), preferred_element_type=f32
-    )
-    copies[2].wait()
-    parts = parts + lax.dot_general(
-        hidden[0], held[2][...], (((0,), (0,)), ((), ())), preferred_element_type=f32
-    )
-    out[...] = parts.astype(bf16)
+    @pl.when(pl.program_id(0) == pl.num_programs(0) - 1)
+    def _():
+        fetch.wait()
 
 
 def loss_kernel(place, parts, noisy, target, modulation, info, message):
@@ -287,54 +276,55 @@
     shape = jax.ShapeDtypeStruct
     params = pltpu.CompilerParams(vmem_limit_bytes=VMEM)
     call = functools.partial(pl.pallas_call, compiler_params=params)
-    other_up = swap_cores(up_weight)
     other_down = swap_cores(down_weight)
+    other_up = swap_cores(up_weight.T).T
+
     member = lax.axis_index("zi") * inner_y + lax.axis_index("yi")
     place = jnp.stack([lax.axis_index("c"), lax.axis_index("x"), member]).astype(jnp.int32)
+    whole = pl.BlockSpec(memory_space=pltpu.VMEM)
     steps = 2
     tile = rows_per // steps
     latent = pl.BlockSpec((1, tile, features), lambda i, place, strata: (place[0], i, 0))
     fixed = lambda array: pl.BlockSpec(array.shape, lambda i, *_: (0,) * len(array.shape))
     kept_rows = shape((share, features), f32)
     levels = shape((2, GROUP, LANES), f32)
-    modulated, info, noisy, target = call(
+    modulated, info, noisy, target, up_near, rows_near = call(
         modulate_kernel,
-        out_shape=(shape((rows_per, features), bf16), levels, kept_rows, kept_rows),
+        out_shape=(
+            shape((rows_per, features), bf16),
+            levels,
+            kept_rows,
+            kept_rows,
+            pltpu.VMEM((units, features), bf16),
+            pltpu.VMEM((rows_per, features), bf16),
+        ),
         grid_spec=pltpu.PrefetchScalarGridSpec(
             num_scalar_prefetch=2,
             grid=(steps,),
-            in_specs=[latent, latent, fixed(modulation)],
+            in_specs=[latent, latent, fixed(modulation), pl.BlockSpec(memory_space=pl.ANY)],
             out_specs=[
                 pl.BlockSpec((tile, features), lambda i, *_: (i, 0)),
                 *(fixed(a) for a in (levels, kept_rows, kept_rows)),
+                whole,
+                whole,
             ],
+            scratch_shapes=[pltpu.SemaphoreType.DMA(())],
         ),
         name="modulate",
-    )(place, *far(strata, clean, noise, modulation))
+    )(place, *far(strata, clean, noise, modulation, up_weight.T))
     members = inner_z * inner_y
     blocks = [modulated] + [
         lax.ppermute(modulated, ("zi", "yi"), [(i, i ^ k) for i in range(members)])
         for k in range(1, members)
     ]
 
-    whole = pl.BlockSpec(memory_space=pltpu.VMEM)
-    away_from = pl.BlockSpec(memory_space=pl.ANY)
-    ups, downs = (up_weight.T, other_up.T), (down_weight, other_down)
-    preact = pltpu.VMEM((units, rows_per), f32)
-    forward = call(
-        forward_kernel,
-        out_shape=(pltpu.VMEM((rows_per, features), bf16), preact, preact),
-        in_specs=[whole, away_from, away_from, away_from, whole],
-        scratch_shapes=[
-            *(pltpu.VMEM((units, features), bf16) for _ in range(3)),
-            pltpu.SemaphoreType.DMA((3,)),
-        ],
-        name="forward",
-    )
-    partial_value, *preacts = forward(
-        modulated, *far(*ups, down_weight), *near(other_down)
-    )
-    parts = exchanged(partial_value.reshape(size_x, share, features), "x")
+    ups, downs = (up_near.T, other_up), (down_weight, other_down)
+    preacts = [jnp.dot(rows_near, w, preferred_element_type=f32) for w in ups]
+    partial_value = sum(
+        jnp.dot(gelu_tanh(p).astype(bf16), w, preferred_element_type=f32)
+        for p, w in zip(preacts, downs)
+    )
+    parts = exchanged(partial_value.astype(bf16).reshape(size_x, share, features), "x")
 
     scalar = pl.BlockSpec(memory_space=pltpu.SMEM)
     loss_call = call(
@@ -354,7 +344,7 @@
         scratch_shapes=[pltpu.VMEM((2 * units + GROUP, rows_per), f32)],
         name="backward",
     )
-    pre_slope = backward(*near(message, *downs, *preacts, info))
+    pre_slope = backward(*near(message, *downs, *(p.T for p in preacts), info))
     pre_slope = exchanged(pre_slope, ("zi", "yi"))
 
     pre_slope, *blocks = near(pre_slope, *blocks)

time: 156 us -> 156 us (level)
  local copies, waits for them, and re-layouts: 2.67 us -> 10.4 us
  waiting for transfers between devices: 31.5 us -> 23.8 us
  Pallas kernels: 16.1 us -> 10.3 us
  matrix products: 0 us -> 5.45 us
    unnamed x12 -> x30, local copies, waits for them, and re-layouts: 2.67 us -> 10.4 us
    pallas_call x2 -> x1, Pallas kernels: 9.02 us -> 2.11 us  [local(): pre_slope = backward(*near(message, *downs, *(p.T for p in preacts), info))]
    ppermute x3, waiting for transfers between devices: 8.09 us -> 2.47 us  [swap_cores(): return lax.ppermute(array, 'c', [(0, 1), (1, 0)])]
    dot_general x0 -> x4, matrix products: none -> 5.45 us  [the longest x2 3.94 us: local(): preacts = [jnp.dot(rows_near, w, preferred_element_type=f32) for w in ups]]
    ppermute x3, waiting for transfers between devices: 23.4 us -> 21.3 us  [local(): lax.ppermute(modulated, ('zi', 'yi'), [(i, i ^ k) for i in range(members)])]
  transfers between devices with their start and end apart: 7 -> 7, of which waited for: 6 -> 4; matrix products, arithmetic and copies ran while one was open for 0% -> 3% of each run, Pallas kernels for 2% -> 2%
where the time goes in v5:
time: 156 us; the launch traced here: 155 us
  blocking collectives  77.6 us (50%)
  starting transfers between devices  26.9 us (17%)
  waiting for transfers between devices  23.8 us (15%)
  local copies, waits for them, and re-layouts  10.4 us (7%)
  Pallas kernels  10.3 us (7%)
  matrix products  5.45 us (3%)
    all_to_all x4, blocking collectives, exchanged(): return lax.all_to_all(array, axis, 0, 0, tiled=True)  77.6 us
    ppermute x3, waiting for transfers between devices, local(): lax.ppermute(modulated, ('zi', 'yi'), [(i, i ^ k) for i in range(members)])  21.3 us
    all_to_all x1, starting transfers between devices, exchanged(): return lax.all_to_all(array, axis, 0, 0, tiled=True)  11.4 us
    unnamed x30, local copies, waits for them, and re-layouts  10.4 us
    ppermute x3, starting transfers between devices, local(): lax.ppermute(modulated, ('zi', 'yi'), [(i, i ^ k) for i in range(members)])  9.2 us
    ppermute x3, starting transfers between devices, swap_cores(): return lax.ppermute(array, 'c', [(0, 1), (1, 0)])  6.25 us
    dot_general x2, matrix products, local(): preacts = [jnp.dot(rows_near, w, preferred_element_type=f32) for w in ups]  3.94 us
    pallas_call x1, Pallas kernels, local(): call(modulate_kernel, out_shape=(shape((rows_per, features), bf16), level...  3.73 us
  transfers between devices with their start and end apart: 7, of which 4 were waited for; matrix products, arithmetic and copies ran while one was open for 3% of the time, Pallas kernels for 2%

profile of v5, /device:TPU:8, one launch (start us, length us, event | category | flops | bytes accessed | tf_op | source)
XLA Modules:
  0.0 155.2 jit_solution(9133886167467778951)
XLA Ops:
  0.6 1.9 %collective-permute-start = (bf16[672,2432]{1,0:T(8,128)(2,1)}, bf16[672,2432]{1,0:T(8,128)(2,1)}, u32[]{:S(2)}, u32[]{:S(2)}) collective-permute-start(bf16[672,2432]{1,0:T(8,128)(2,1)} %bitcast.18), channel_id=1, source_target_pairs={{0,1},{1,0},{2,3},{3,2},{4,5},{5,4},{6,7},{7,6},{8,9},{9,8},{10,11... | collective-permute-start | bytes 9805832 | tf_op jit(solution)/shard_map/ppermute | solution.py:35
  2.6 2.4 %collective-permute-start.1 = (bf16[672,2432]{1,0:T(8,128)(2,1)}, bf16[672,2432]{1,0:T(8,128)(2,1)S(1)}, u32[]{:S(2)}, u32[]{:S(2)}) collective-permute-start(bf16[672,2432]{1,0:T(8,128)(2,1)} %down_0.1), channel_id=1, source_target_pairs={{0,1},{1,0},{2,3},{3,2},{4,5},{5,4},{6,7},{7,6},{8,9},{9,8},{10,11... | collective-permute-start | bytes 9805832 | tf_op jit(solution)/shard_map/ppermute | solution.py:35
  5.1 3.7 %modulate.1 = (bf16[128,2432]{1,0:T(8,128)(2,1)S(1)}, f32[2,8,128]{2,1,0:T(8,128)S(1)}, f32[32,2432]{1,0:T(8,128)S(1)}, f32[32,2432]{1,0:T(8,128)S(1)}, bf16[672...) custom-call(s32[3]{0:T(128)S(1)} %pad_add_fusion.place, s32[2]{0:T(128)} %strata.1, bf16[2,128,2432]{2,1,0:T(8,128)(2,1)} %clean.1, ...), custom_call_target="tpu_custom_call" | custom-call | tf_op jit(solution)/shard_map/modulate/pallas_call | solution.py:291
  8.8 0.9 copy-done.1
  9.7 1.0 fusion.36
  10.7 0.9 copy-done
  12.4 2.9 %fusion.37 = f32[128,672]{0,1:T(8,128)S(1)} fusion(bf16[128,2432]{1,0:T(8,128)(2,1)S(1)} %get-tuple-element.10, bf16[672,2432]{1,0:T(8,128)(2,1)} %collective-permute-done), kind=kOutput, calls=%fused_computation.39 | convolution fusion | flops 418381824 | bytes 4235264 | tf_op jit(solution)/shard_map/dot_general | solution.py:322
  16.1 14.8 %all_to_all.25.parts = bf16[4,32,2432]{2,1,0:T(8,128)(2,1)S(1)} all-to-all(bf16[4,32,2432]{2,1,0:T(8,128)(2,1)S(1)} %bitcast.20), channel_id=1, replica_groups=mesh['zb'=6,'zi'=2,'yb'=4,'yi'=2,'x'=4,'c'=2] {'x'}, dimensions={0} | all-to-all | bytes 1245184 | tf_op jit(solution)/shard_map/all_to_all | solution.py:39
  30.9 0.9 loss.1
  31.8 12.6 %all_to_all.26.message = bf16[4,32,2560]{2,1,0:T(8,128)(2,1)S(1)} all-to-all(bf16[4,32,2560]{2,1,0:T(8,128)(2,1)S(1)} %loss.1), channel_id=1, replica_groups=mesh['zb'=6,'zi'=2,'yb'=4,'yi'=2,'x'=4,'c'=2] {'x'}, dimensions={0} | all-to-all | bytes 1310720 | tf_op jit(solution)/shard_map/all_to_all | solution.py:39
  44.4 2.1 %backward.1 = bf16[4,384,128]{2,1,0:T(8,128)(2,1)S(1)} custom-call(bf16[4,32,2560]{2,1,0:T(8,128)(2,1)S(1)} %all_to_all.26.message, bf16[672,2432]{1,0:T(8,128)(2,1)S(1)} %copy-done, bf16[672,2432]{1,0:T(8,128)(2,1)S(1)} %collective-permute-done.1.down_1, f32[672,128]{1,0:T(8,128)S(1)} %bitcast.16, f32[672,128]{1,0:T(8,128)S(1)} %bitcast.17, ...), custom_call_target="tpu_custom_call" | custom-call | tf_op jit(solution)/shard_map/backward/pallas_call | solution.py:347
  47.3 11.4 %all-to-all-start.2 = ((bf16[4,384,128]{2,1,0:T(8,128)(2,1)}), bf16[4,384,128]{2,1,0:T(8,128)(2,1)S(1)}, u32[]{:S(2)}, u32[]{:S(2)}) async-start(bf16[4,384,128]{2,1,0:T(8,128)(2,1)} %copy-done.13), calls=%async_computation.2 | async-start | bytes 786432 | tf_op jit(solution)/shard_map/all_to_all | solution.py:39
  58.7 1.9 %collective-permute-start.2 = (bf16[128,2432]{1,0:T(8,128)(2,1)}, bf16[128,2432]{1,0:T(8,128)(2,1)S(1)}, u32[]{:S(2)}, u32[]{:S(2)}) collective-permute-start(bf16[128,2432]{1,0:T(8,128)(2,1)} %copy-done.1), channel_id=1, source_target_pairs={{0,8},{8,0},{64,72},{72,64},{1,9},{9,1},{65,73},{73,65},{2,10},{10... | collective-permute-start | bytes 1867784 | tf_op jit(solution)/shard_map/ppermute | solution.py:317
  60.6 3.9 %collective-permute-start.3 = (bf16[128,2432]{1,0:T(8,128)(2,1)}, bf16[128,2432]{1,0:T(8,128)(2,1)S(1)}, u32[]{:S(2)}, u32[]{:S(2)}) collective-permute-start(bf16[128,2432]{1,0:T(8,128)(2,1)} %copy-done.1), channel_id=1, source_target_pairs={{0,64},{8,72},{64,0},{72,8},{1,65},{9,73},{65,1},{73,9},{2,66},{10... | collective-permute-start | bytes 1867784 | tf_op jit(solution)/shard_map/ppermute | solution.py:317
  64.5 3.4 %collective-permute-start.4 = (bf16[128,2432]{1,0:T(8,128)(2,1)}, bf16[128,2432]{1,0:T(8,128)(2,1)S(1)}, u32[]{:S(2)}, u32[]{:S(2)}) collective-permute-start(bf16[128,2432]{1,0:T(8,128)(2,1)} %copy-done.1), channel_id=1, source_target_pairs={{0,72},{8,64},{64,8},{72,0},{1,73},{9,65},{65,9},{73,1},{2,74},{10... | collective-permute-start | bytes 1867784 | tf_op jit(solution)/shard_map/ppermute | solution.py:317
  67.9 9.9 %collective-permute-done.2.refs_1_ = bf16[128,2432]{1,0:T(8,128)(2,1)S(1)} collective-permute-done((bf16[128,2432]{1,0:T(8,128)(2,1)}, bf16[128,2432]{1,0:T(8,128)(2,1)S(1)}, u32[]{:S(2)}, u32[]{:S(2)}) %collective-permute-start.2) | collective-permute-done | bytes 622624 | tf_op jit(solution)/shard_map/ppermute | solution.py:317
  77.8 0.8 copy-done.4
  78.6 1.0 collective-permute-done.3.refs_2_
  79.6 0.8 copy-done.7
  80.5 10.4 %collective-permute-done.4.refs_3_ = bf16[128,2432]{1,0:T(8,128)(2,1)S(1)} collective-permute-done((bf16[128,2432]{1,0:T(8,128)(2,1)}, bf16[128,2432]{1,0:T(8,128)(2,1)S(1)}, u32[]{:S(2)}, u32[]{:S(2)}) %collective-permute-start.4) | collective-permute-done | bytes 622624 | tf_op jit(solution)/shard_map/ppermute | solution.py:317
  90.9 0.9 copy-done.10
  91.7 1.1 copy-done.2
  92.8 1.1 copy-done.5
  93.9 1.1 copy-done.8
  95.0 1.1 copy-done.11
  96.1 1.2 away.1
  97.3 1.9 %collective-permute-start.5 = (bf16[192,2432]{1,0:T(8,128)(2,1)S(1)}, bf16[192,2432]{1,0:T(8,128)(2,1)S(1)}, u32[]{:S(2)}, u32[]{:S(2)}) collective-permute-start(bf16[192,2432]{1,0:T(8,128)(2,1)S(1)} %away.1), channel_id=1, source_target_pairs={{0,1},{1,0},{2,3},{3,2},{4,5},{5,4},{6,7},{7,6},{8,9},{9,8},{10,11... | collective-permute-start | bytes 2801672 | tf_op jit(solution)/shard_map/ppermute | solution.py:35
  99.2 2.5 %collective-permute-done.5.got = bf16[192,2432]{1,0:T(8,128)(2,1)S(1)} collective-permute-done((bf16[192,2432]{1,0:T(8,128)(2,1)S(1)}, bf16[192,2432]{1,0:T(8,128)(2,1)S(1)}, u32[]{:S(2)}, u32[]{:S(2)}) %collective-permute-start.5) | collective-permute-done | bytes 933920 | tf_op jit(solution)/shard_map/ppermute | solution.py:35
  101.7 1.1 copy-done.3
  102.8 1.4 home.1
  104.1 26.9 %all_to_all.27.parts = bf16[4,816,128]{2,1,0:T(8,128)(2,1)S(1)} all-to-all(bf16[4,816,128]{2,1,0:T(8,128)(2,1)S(1)} %bitcast.15), channel_id=1, replica_groups=mesh['zb'=6,'zi'=2,'yb'=4,'yi'=2,'x'=4,'c'=2] {'yb'}, dimensions={0} | all-to-all | bytes 1671168 | tf_op jit(solution)/shard_map/all_to_all | solution.py:39
  131.2 23.3 %all_to_all.28.parts = bf16[6,136,128]{2,1,0:T(8,128)(2,1)S(1)} all-to-all(bf16[6,136,128]{2,1,0:T(8,128)(2,1)S(1)} %middle.1), channel_id=1, replica_groups=mesh['zb'=6,'zi'=2,'yb'=4,'yi'=2,'x'=4,'c'=2] {'zb'}, dimensions={0} | all-to-all | bytes 417792 | tf_op jit(solution)/shard_map/all_to_all | solution.py:39
  (28 shorter events, 3.3 us)
Async XLA Ops:
  0.6 11.7 %collective-permute-start = (bf16[672,2432]{1,0:T(8,128)(2,1)}, bf16[672,2432]{1,0:T(8,128)(2,1)}, u32[]{:S(2)}, u32[]{:S(2)}) collective-permute-start(bf16[672,2432]{1,0:T(8,128)(2,1)} %bitcast.18), channel_id=1, source_target_pairs={{0,1},{1,0},{2,3},{3,2},{4,5},{5,4},{6,7},{7,6},{8,9},{9,8},{10,11... | collective-permute-start | bytes 9805832 | tf_op jit(solution)/shard_map/ppermute | solution.py:35
  2.6 12.7 %collective-permute-start.1 = (bf16[672,2432]{1,0:T(8,128)(2,1)}, bf16[672,2432]{1,0:T(8,128)(2,1)S(1)}, u32[]{:S(2)}, u32[]{:S(2)}) collective-permute-start(bf16[672,2432]{1,0:T(8,128)(2,1)} %down_0.1), channel_id=1, source_target_pairs={{0,1},{1,0},{2,3},{3,2},{4,5},{5,4},{6,7},{7,6},{8,9},{9,8},{10,11... | collective-permute-start | bytes 9805832 | tf_op jit(solution)/shard_map/ppermute | solution.py:35
  8.8 0.9 copy-start.1
  9.7 1.9 %copy-start = (bf16[672,2432]{1,0:T(8,128)(2,1)S(1)}, bf16[672,2432]{1,0:T(8,128)(2,1)}, u32[]{:S(2)}) copy-start(bf16[672,2432]{1,0:T(8,128)(2,1)} %down_0.1) | copy-start | bytes 9805828
  15.3 15.6 %copy-start.14 = (f32[2,7296]{1,0:T(2,128)S(1)}, f32[2,7296]{1,0:T(2,128)}, u32[]{:S(2)}) copy-start(f32[2,7296]{1,0:T(2,128)} %modulation.3) | copy-start | bytes 175108
  46.5 0.8 copy-start.13
  47.3 44.5 %all-to-all-start.2 = ((bf16[4,384,128]{2,1,0:T(8,128)(2,1)}), bf16[4,384,128]{2,1,0:T(8,128)(2,1)S(1)}, u32[]{:S(2)}, u32[]{:S(2)}) async-start(bf16[4,384,128]{2,1,0:T(8,128)(2,1)} %copy-done.13), calls=%async_computation.2 | async-start | bytes 786432 | tf_op jit(solution)/shard_map/all_to_all | solution.py:39
  58.7 19.1 %collective-permute-start.2 = (bf16[128,2432]{1,0:T(8,128)(2,1)}, bf16[128,2432]{1,0:T(8,128)(2,1)S(1)}, u32[]{:S(2)}, u32[]{:S(2)}) collective-permute-start(bf16[128,2432]{1,0:T(8,128)(2,1)} %copy-done.1), channel_id=1, source_target_pairs={{0,8},{8,0},{64,72},{72,64},{1,9},{9,1},{65,73},{73,65},{2,10},{10... | collective-permute-start | bytes 1867784 | tf_op jit(solution)/shard_map/ppermute | solution.py:317
  60.6 19.0 %collective-permute-start.3 = (bf16[128,2432]{1,0:T(8,128)(2,1)}, bf16[128,2432]{1,0:T(8,128)(2,1)S(1)}, u32[]{:S(2)}, u32[]{:S(2)}) collective-permute-start(bf16[128,2432]{1,0:T(8,128)(2,1)} %copy-done.1), channel_id=1, source_target_pairs={{0,64},{8,72},{64,0},{72,8},{1,65},{9,73},{65,1},{73,9},{2,66},{10... | collective-permute-start | bytes 1867784 | tf_op jit(solution)/shard_map/ppermute | solution.py:317
  64.5 26.4 %collective-permute-start.4 = (bf16[128,2432]{1,0:T(8,128)(2,1)}, bf16[128,2432]{1,0:T(8,128)(2,1)S(1)}, u32[]{:S(2)}, u32[]{:S(2)}) collective-permute-start(bf16[128,2432]{1,0:T(8,128)(2,1)} %copy-done.1), channel_id=1, source_target_pairs={{0,72},{8,64},{64,8},{72,0},{1,73},{9,65},{65,9},{73,1},{2,74},{10... | collective-permute-start | bytes 1867784 | tf_op jit(solution)/shard_map/ppermute | solution.py:317
  77.8 0.8 copy-start.4
  79.6 0.8 copy-start.7
  90.9 0.9 copy-start.10
  91.7 1.1 copy-start.2
  92.8 1.1 copy-start.5
  93.9 1.1 copy-start.8
  95.0 1.1 copy-start.11
  96.0 5.6 %copy-start.6 = (bf16[128,2432]{1,0:T(8,128)(2,1)S(1)}, bf16[128,2432]{1,0:T(8,128)(2,1)}, u32[]{:S(2)}) copy-start(bf16[128,2432]{1,0:T(8,128)(2,1)} %copy-done.4) | copy-start | bytes 1867780
  96.0 5.6 %copy-start.9 = (bf16[128,2432]{1,0:T(8,128)(2,1)S(1)}, bf16[128,2432]{1,0:T(8,128)(2,1)}, u32[]{:S(2)}) copy-start(bf16[128,2432]{1,0:T(8,128)(2,1)} %copy-done.7) | copy-start | bytes 1867780
  96.1 5.6 %copy-start.12 = (bf16[128,2432]{1,0:T(8,128)(2,1)S(1)}, bf16[128,2432]{1,0:T(8,128)(2,1)}, u32[]{:S(2)}) copy-start(bf16[128,2432]{1,0:T(8,128)(2,1)} %copy-done.10) | copy-start | bytes 1867780
  97.3 4.4 %collective-permute-start.5 = (bf16[192,2432]{1,0:T(8,128)(2,1)S(1)}, bf16[192,2432]{1,0:T(8,128)(2,1)S(1)}, u32[]{:S(2)}, u32[]{:S(2)}) collective-permute-start(bf16[192,2432]{1,0:T(8,128)(2,1)S(1)} %away.1), channel_id=1, source_target_pairs={{0,1},{1,0},{2,3},{3,2},{4,5},{5,4},{6,7},{7,6},{8,9},{9,8},{10,11... | collective-permute-start | bytes 2801672 | tf_op jit(solution)/shard_map/ppermute | solution.py:35
  101.7 1.1 copy-start.3
